TPU v7x, 512 devices: a whole 4x4x16 slice. The times are simulated.
512 devices in a mesh: rep: 4 (over y), fsdp: 128 (over x, z, core).
Axes of the slice: x: 4, y: 4, z: 16, core: 2. Of those that a mesh axis runs over, the one named last changes fastest.
Arguments:
- momentum: float32 [4, 18432, 2304], P('rep', 'fsdp'), may hold values from -60 to 60
- gradient: bfloat16 [4, 18432, 2304], P('rep', 'fsdp'), may hold values from -30 to 30
- right_factor: float32 [2304, 256], P('fsdp'), may hold values from -0.125 to 0.125
Outputs:
- new_momentum: float32 [4, 18432, 2304], P('rep', 'fsdp')
- update: bfloat16 [18432, 2304], P('fsdp')
- new_factor: float32 [2304, 256], P('fsdp')
All inputs are finite; a program needn't handle non-finite values.
Results may differ from a plain program's by a relative error of at most 0.001.
Values sent between devices are 32-bit elements; how exact they have to be, the bound alone decides.
A program may use at most 64 MiB of HBM per device.

v0:
```python
import math

import jax
import jax.numpy as jnp
from jax import lax
from jax.sharding import Mesh
from jax.sharding import PartitionSpec as P

ROWS = 18432
COLS = 2304
RANK = 256
FSDP = ("fsdp_0", "fsdp_1", "fsdp_2")


epsilon = 1e-06
decay_rate = 0.95
highest = lax.Precision.HIGHEST


def sent_to_all(shard, axis):
    devices = lax.axis_size(axis)
    return lax.all_to_all(
        jnp.broadcast_to(shard[None], (devices, *shard.shape)), axis, 0, 0, tiled=True
    )


def joined_along(parts, dim):
    lengths = list(parts.shape[1:])
    lengths[dim] *= parts.shape[0]
    return jnp.moveaxis(parts, 0, dim).reshape(lengths)


def whole_of(shard, axes, dim):
    far, near = axes
    first = sent_to_all(shard, far)
    parts = jnp.swapaxes(sent_to_all(first, near), 0, 1)
    return joined_along(parts.reshape(-1, *shard.shape), dim)


def of_everyone(shard, axis):
    everything = sent_to_all(shard, axis)
    return jnp.sum(everything, axis=0)


def split_up(shard, dim, devices):
    before, after = (shard.shape[:dim], shard.shape[dim + 1 :])
    return jnp.moveaxis(shard.reshape(*before, devices, -1, *after), dim, 0)


def summed_on_arrival(shard, axis, dim):
    devices = lax.axis_size(axis)
    parts = lax.all_to_all(split_up(shard, dim, devices), axis, 0, 0, tiled=True)
    return jnp.sum(parts, axis=0)


def sum_by_axis(shard, axes, dim):
    far, near = axes
    parts = split_up(shard, dim, lax.axis_size(far))
    nearer = summed_on_arrival(parts, near, dim + 1)
    arrived = lax.all_to_all(nearer, far, split_axis=0, concat_axis=0, tiled=True)
    return arrived.sum(axis=0)


def rows_for(lines, devices):
    spare = -lines.shape[0] % devices
    if not spare:
        return lines
    return jnp.concatenate([lines, jnp.zeros((spare, *lines.shape[1:]), lines.dtype)])


def total_of(shard, axes):
    lines = shard.reshape(-1, shard.shape[-1])
    own = sum_by_axis(rows_for(lines, lax.axis_size(axes[0]) * lax.axis_size(axes[1])), axes, 0)
    whole = whole_of(own, axes, 0)
    return whole[: len(lines)].reshape(shard.shape)


def sum_by_parts(shard, axes):
    lines = shard.reshape(-1)
    own = sum_by_axis(rows_for(lines, lax.axis_size(axes[0]) * lax.axis_size(axes[1])), axes, 0)
    whole = whole_of(own, axes, 0)
    return whole[: len(lines)].reshape(shard.shape)


def shards(momentum, gradient, right_factor):
    buffer = momentum[0] + gradient[0].astype(jnp.float32)
    replicas = lax.axis_size("rep")
    shard_rows = COLS // lax.axis_size(FSDP)
    columns = buffer
    partial_left = jnp.dot(
        columns,
        whole_of(right_factor, (("fsdp_0", "fsdp_1"), "fsdp_2"), 0),
        precision=highest,
        preferred_element_type=jnp.float32,
    )
    projected = of_everyone(partial_left, "rep")
    local_gram = jnp.dot(
        projected.T, projected, precision=highest, preferred_element_type=jnp.float32
    )
    gram_matrix = total_of(local_gram, (("fsdp_0", "fsdp_1"), "fsdp_2"))
    lower_factor = jnp.linalg.cholesky(gram_matrix)
    orthonormal = jax.scipy.linalg.solve_triangular(lower_factor, projected.T, lower=True).T
    columns = buffer
    full_factor = (
        sum_by_parts(
            lax.dot_general(
                columns,
                orthonormal,
                (((0,), (0,)), ((), ())),
                precision=highest,
                preferred_element_type=jnp.float32,
            ),
            (("rep", "fsdp_0"), ("fsdp_1", "fsdp_2")),
        )
        / replicas
    )
    col_norms = jnp.sqrt(jnp.sum(full_factor * full_factor, axis=0) + epsilon)
    own_factor = lax.dynamic_slice_in_dim(
        full_factor, lax.axis_index(FSDP) * shard_rows, shard_rows, 0
    )
    new_factor = own_factor / col_norms
    correction = lax.dot_general(
        orthonormal,
        full_factor,
        (((1,), (1,)), ((), ())),
        precision=highest,
        preferred_element_type=jnp.float32,
    )
    new_momentum = (buffer - (1.0 - decay_rate) * correction)[None]
    direction = lax.dot_general(
        orthonormal,
        full_factor / col_norms,
        (((1,), (1,)), ((), ())),
        precision=highest,
        preferred_element_type=jnp.float32,
    )
    update = (math.sqrt(ROWS * COLS / RANK) * direction).astype(jnp.bfloat16)
    return (new_momentum, update, new_factor)


def solution(mesh):
    split = Mesh(
        mesh.devices.reshape(mesh.shape["rep"], 4, 16, 2), ("rep", "fsdp_0", "fsdp_1", "fsdp_2")
    )
    in_specs = (P("rep", FSDP, None), P("rep", FSDP, None), P(FSDP, None))
    out_specs = (P("rep", FSDP, None), P(FSDP, None), P(FSDP, None))
    return jax.shard_map(
        shards, mesh=split, in_specs=in_specs, out_specs=out_specs, check_vma=False
    )
```

profile of v0, /device:TPU:1, one launch (start us, length us, event | category | flops | bytes accessed | tf_op | source)
XLA Modules:
  0.0 518.0 jit_solution(15678474658383538471)
XLA Ops:
  0.6 0.8 broadcast_in_dim.19
  1.5 89.3 %all_to_all.60 = f32[64,18,256]{2,1,0:T(8,128)S(1)} all-to-all(f32[64,18,256]{2,1,0:T(8,128)S(1)} %broadcast_in_dim.19), channel_id=1, replica_groups=mesh['rep'=4,'fsdp_0'=4,'fsdp_1'=16,'fsdp_2'=2] {'fsdp_0','fsdp_1'}, dimensions={0} | all-to-all | bytes 2359296 | tf_op jit(solution)/shard_map/all_to_all | solution.py:22
  90.8 0.4 copy.32
  91.2 0.3 broadcast_in_dim.20
  91.5 12.0 %all_to_all.61 = f32[2,64,18,256]{3,1,2,0:T(8,128)S(1)} all-to-all(f32[2,64,18,256]{3,1,2,0:T(8,128)S(1)} %broadcast_in_dim.20), channel_id=1, replica_groups=mesh['rep'=4,'fsdp_0'=4,'fsdp_1'=16,'fsdp_2'=2] {'fsdp_2'}, dimensions={0} | all-to-all | bytes 4718592 | tf_op jit(solution)/shard_map/all_to_all | solution.py:22
  103.5 1.4 copy.33
  104.9 1.6 reshape_reshape.7
  106.5 3.7 fusion.6
  110.2 13.6 %all_to_all.62 = f32[4,144,256]{2,1,0:T(8,128)S(1)} all-to-all(f32[4,144,256]{2,1,0:T(8,128)S(1)} %broadcast_in_dim.22), channel_id=1, replica_groups=mesh['rep'=4,'fsdp_0'=4,'fsdp_1'=16,'fsdp_2'=2] {'rep'}, dimensions={0} | all-to-all | bytes 1179648 | tf_op jit(solution)/shard_map/all_to_all | solution.py:22
  124.2 0.4 convolution_bitcast_fusion
  124.5 5.1 all_to_all.63
  129.8 20.9 %all_to_all.64 = f32[64,2,256]{2,1,0:T(2,128)S(1)} all-to-all(f32[64,2,256]{2,1,0:T(2,128)S(1)} %copy.36), channel_id=1, replica_groups=mesh['rep'=4,'fsdp_0'=4,'fsdp_1'=16,'fsdp_2'=2] {'fsdp_0','fsdp_1'}, dimensions={0} | all-to-all | bytes 262144 | tf_op jit(solution)/shard_map/all_to_all | solution.py:60
  150.7 0.7 broadcast_in_dim.23
  151.4 7.3 %all-to-all-start.5 = ((f32[64,2,256]{2,1,0:T(2,128)}), f32[64,2,256]{2,1,0:T(2,128)S(1)}, u32[]{:S(2)}, u32[]{:S(2)}) async-start(f32[64,2,256]{2,1,0:T(2,128)} %broadcast_in_dim.23), calls=%async_computation.5 | async-start | bytes 262144 | tf_op jit(solution)/shard_map/all_to_all | solution.py:22
  158.7 14.0 %all-to-all-done.5 = f32[64,2,256]{2,1,0:T(2,128)S(1)} async-done(((f32[64,2,256]{2,1,0:T(2,128)}), f32[64,2,256]{2,1,0:T(2,128)S(1)}, u32[]{:S(2)}, u32[]{:S(2)}) %all-to-all-start.5) | async-done | bytes 131104 | tf_op jit(solution)/shard_map/all_to_all | solution.py:22
  172.8 6.9 %all_to_all.65 = f32[2,64,2,256]{3,2,1,0:T(2,128)S(1)} all-to-all(f32[2,64,2,256]{3,2,1,0:T(2,128)S(1)} %broadcast_in_dim.24), channel_id=1, replica_groups=mesh['rep'=4,'fsdp_0'=4,'fsdp_1'=16,'fsdp_2'=2] {'fsdp_2'}, dimensions={0} | all-to-all | bytes 524288 | tf_op jit(solution)/shard_map/all_to_all | solution.py:22
  179.8 0.2 reshape_reshape.8
  180.2 11.7 %cholesky.50 = f32[128,128]{1,0:T(8,128)S(1)} custom-call(f32[128,128]{1,0:T(8,128)S(1)} %cholesky.118), custom_call_target="Cholesky" | custom-call | tf_op jit(solution)/shard_map/jit(cholesky)/cholesky | solution.py:101
  192.0 9.8 %custom-call.15 = f32[1,128,128]{1,2,0:T(8,128)S(1)} custom-call(f32[1,128,128]{2,1,0:T(8,128)S(1)} %get-tuple-element.24), custom_call_target="InvertDiagBlocksLowerTriangular" | custom-call | tf_op jit(solution)/shard_map/jit(cholesky)/cholesky | solution.py:101
  201.8 0.2 constant_dynamic-update-slice_fusion
  202.0 0.3 convolution_subtract_fusion.1
  202.3 11.7 %cholesky.105 = f32[128,128]{1,0:T(8,128)S(1)} custom-call(f32[128,128]{1,0:T(8,128)S(1)} %convolution_subtract_fusion.1), custom_call_target="Cholesky" | custom-call | tf_op jit(solution)/shard_map/jit(cholesky)/cholesky | solution.py:101
  214.0 0.6 compare_reduce_fusion
  216.1 4.0 while.1
  216.1 0.6 fusion.30
  216.7 1.4 bitcast_dynamic-update-slice_fusion.2
  218.1 0.6 fusion.30
  218.7 1.4 bitcast_dynamic-update-slice_fusion.2
  220.1 19.9 %custom-call.16 = f32[2,128,128]{1,2,0:T(8,128)S(1)} custom-call(f32[2,128,128]{2,1,0:T(8,128)S(1)} %get-tuple-element.10), custom_call_target="InvertDiagBlocksLowerTriangular" | custom-call | tf_op jit(solution)/shard_map/jit(_solve_triangular)/triangular_solve | solution.py:102
  240.0 0.2 fusion.12
  240.2 0.3 convolution_subtract_fusion
  240.5 0.2 fusion.15
  240.7 5.3 %fusion.4 = f32[2304,256]{1,0:T(8,128)} fusion(f32[1,144,2304]{2,1,0:T(8,128)S(1)} %copy-done, bf16[1,144,2304]{2,1,0:T(8,128)(2,1)S(1)} %copy-done.2, f32[128,144]{0,1:T(8,128)S(1)} %fusion.15, f32[128,144]{0,1:T(8,128)S(1)} %fusion.12), kind=kOutput, calls=%fused_computation.11 | convolution fusion | flops 1019916288 | bytes 4497408 | tf_op jit(solution)/shard_map/dot_general | solution.py:106
  246.0 2.5 reshape_reshape_reshape.4
  248.5 1.4 copy.47
  249.9 116.3 %all_to_all.66 = f32[32,16,1152]{2,1,0:T(8,128)S(1)} all-to-all(f32[32,16,1152]{2,1,0:T(8,128)S(1)} %bitcast.59), channel_id=1, replica_groups=mesh['rep'=4,'fsdp_0'=4,'fsdp_1'=16,'fsdp_2'=2] {'fsdp_1','fsdp_2'}, dimensions={0} | all-to-all | bytes 4718592 | tf_op jit(solution)/shard_map/all_to_all | solution.py:52
  366.4 9.4 %all_to_all.67 = f32[16,1,1152]{2,1,0:T(1,128)S(1)} all-to-all(f32[16,1,1152]{2,1,0:T(1,128)S(1)} %all_to_all.45), channel_id=1, replica_groups=mesh['rep'=4,'fsdp_0'=4,'fsdp_1'=16,'fsdp_2'=2] {'rep','fsdp_0'}, dimensions={0} | all-to-all | bytes 147456 | tf_op jit(solution)/shard_map/all_to_all | solution.py:60
  376.0 9.7 %all_to_all.68 = f32[16,1,1152]{2,1,0:T(1,128)S(1)} all-to-all(f32[16,1,1152]{2,1,0:T(1,128)S(1)} %broadcast_in_dim.25), channel_id=1, replica_groups=mesh['rep'=4,'fsdp_0'=4,'fsdp_1'=16,'fsdp_2'=2] {'rep','fsdp_0'}, dimensions={0} | all-to-all | bytes 147456 | tf_op jit(solution)/shard_map/all_to_all | solution.py:22
  385.7 1.6 broadcast_in_dim.27
  387.3 6.7 %all-to-all-start.10 = ((f32[32,16,1152]{2,1,0:T(8,128)}), f32[32,16,1152]{2,1,0:T(8,128)S(1)}, u32[]{:S(2)}, u32[]{:S(2)}) async-start(f32[32,16,1152]{2,1,0:T(8,128)} %broadcast_in_dim.27), calls=%async_computation.10 | async-start | bytes 4718592 | tf_op jit(solution)/shard_map/all_to_all | solution.py:22
  394.0 110.2 %all-to-all-done.10 = f32[32,16,1152]{2,1,0:T(8,128)S(1)} async-done(((f32[32,16,1152]{2,1,0:T(8,128)}), f32[32,16,1152]{2,1,0:T(8,128)S(1)}, u32[]{:S(2)}, u32[]{:S(2)}) %all-to-all-start.10) | async-done | bytes 2359328 | tf_op jit(solution)/shard_map/all_to_all | solution.py:22
  504.3 2.1 copy.40
  506.4 2.5 div.39
  509.0 0.3 multiply_reduce_fusion
  509.3 1.0 copy-done.1
  510.3 3.7 fusion.1
  514.0 3.4 fusion.2
  517.4 0.6 dynamic-slice_divide_fusion
  (33 shorter events, 1.5 us)
Async XLA Ops:
  151.4 21.3 %all-to-all-start.5 = ((f32[64,2,256]{2,1,0:T(2,128)}), f32[64,2,256]{2,1,0:T(2,128)S(1)}, u32[]{:S(2)}, u32[]{:S(2)}) async-start(f32[64,2,256]{2,1,0:T(2,128)} %broadcast_in_dim.23), calls=%async_computation.5 | async-start | bytes 262144 | tf_op jit(solution)/shard_map/all_to_all | solution.py:22
  180.0 60.7 %copy-start = (f32[1,144,2304]{2,1,0:T(8,128)S(1)}, f32[1,144,2304]{2,1,0:T(8,128)}, u32[]{:S(2)}) copy-start(f32[1,144,2304]{2,1,0:T(8,128)} %param.3) | copy-start | bytes 3981316
  180.0 60.7 %copy-start.2 = (bf16[1,144,2304]{2,1,0:T(8,128)(2,1)S(1)}, bf16[1,144,2304]{2,1,0:T(8,128)(2,1)}, u32[]{:S(2)}) copy-start(bf16[1,144,2304]{2,1,0:T(8,128)(2,1)} %param.4) | copy-start | bytes 1990660
  387.3 116.9 %all-to-all-start.10 = ((f32[32,16,1152]{2,1,0:T(8,128)}), f32[32,16,1152]{2,1,0:T(8,128)S(1)}, u32[]{:S(2)}, u32[]{:S(2)}) async-start(f32[32,16,1152]{2,1,0:T(8,128)} %broadcast_in_dim.27), calls=%async_computation.10 | async-start | bytes 4718592 | tf_op jit(solution)/shard_map/all_to_all | solution.py:22
  509.0 1.3 copy-start.1
where the time goes:
time: 519 us; the launch traced here: 518 us
  blocking collectives  283 us (55%)
  waiting for transfers between devices  124 us (24%)
  other arithmetic  55.3 us (11%)
  local copies, waits for them, and re-layouts  21.4 us (4%)
  matrix products  17.6 us (3%)
  starting transfers between devices  14 us (3%)
    all_to_all x5, blocking collectives, sent_to_all(): lax.all_to_all(jnp.broadcast_to(shard[None], (devices, *shard.shape)), ax...  132 us
    all_to_all x2, waiting for transfers between devices, sent_to_all(): lax.all_to_all(jnp.broadcast_to(shard[None], (devices, *shard.shape)), ax...  124 us
    all_to_all x2, blocking collectives, summed_on_arrival(): lax.all_to_all(split_up(shard, dim, devices), axis, 0, 0, tiled=True)  121 us
    another operation x6, other arithmetic, shards(): lower_factor = jnp.linalg.cholesky(gram_matrix)  33.9 us
    all_to_all x2, blocking collectives, sum_by_axis(): lax.all_to_all(nearer, far, split_axis=0, concat_axis=0, tiled=True)  30.3 us
    another operation x3, other arithmetic, shards(): jax.scipy.linalg.solve_triangular(lower_factor, projected.T, lower=True)  19.9 us
    all_to_all x2, starting transfers between devices, sent_to_all(): lax.all_to_all(jnp.broadcast_to(shard[None], (devices, *shard.shape)), ax...  14 us
  transfers between devices with their start and end apart: 2, of which 2 were waited for; matrix products, arithmetic and copies ran while one was open for 0% of the time, Pallas kernels for 0%

commit v1 on v0

v1 whole, which is shorter than its diff:
```python
import math

import jax
import jax.numpy as jnp
from jax import lax
from jax.experimental import pallas as pl
from jax.experimental.pallas import tpu as pltpu
from jax.sharding import Mesh
from jax.sharding import PartitionSpec as P

ROWS = 18432
COLS = 2304
RANK = 256
REPLICAS = 4
FSDP = ("fx", "fz", "fc")

NX, NZ = 4, 16
SHARD = ROWS // 128
BLOCK = COLS // 4
OWN = COLS // 128
PIECE = 80
FACTOR_ROWS = 72
TILES = PIECE // 8

epsilon = 1e-06
decay_rate = 0.95
highest = lax.Precision.HIGHEST
MESH = pl.DeviceIdType.MESH
VMEM = pltpu.VMEM
f32 = jnp.float32


def copy_to(src, dst, send, recv, device):
    return pltpu.make_async_remote_copy(
        src_ref=src,
        dst_ref=dst,
        send_sem=send,
        recv_sem=recv,
        device_id=device,
        device_id_type=MESH,
    )


def gather_ring(block, me, right, left, send, recv):
    before, after, across = (me + 3) % 4, (me + 1) % 4, (me + 2) % 4

    def hop(q, h, device, i):
        return copy_to(block(q, h), block(q, h), send.at[i], recv.at[i], device)

    first = [hop(me, 0, right, 0), hop(me, 1, left, 1), hop(me, 1, right, 2), hop(me, 0, left, 3)]
    for copy in first:
        copy.start()
    first[0].wait_recv()
    onward = hop(before, 0, right, 4)
    onward.start()
    first[1].wait_recv()
    backward = hop(after, 1, left, 5)
    backward.start()
    first[2].wait_recv()
    first[3].wait_recv()
    onward.wait_recv()
    backward.wait_recv()
    for copy in first + [onward, backward]:
        copy.wait_send()


def exchange_kernel(
    m_hbm, g_hbm, r_hbm, p_out, mall,
    mv, gv, bs, raw, comb, cin, inn, s_c, rall, rc, pall, gram, mloc, crecv, mx, xrecv, mz, zrecv, fin,
    load, s_send, s_recv, rx_send, rx_recv, rz_send, rz_recv, rc_send, rc_recv, p_send, p_recv,
    c_send, c_recv, x_send, x_recv, z_send, z_recv, f_send, f_recv, a_send, a_recv, b_send, b_recv,
    d_send, d_recv,
):
    y, x, z, c = (lax.axis_index(name) for name in ("rep",) + FSDP)

    def at_y(q):
        return (q, x, z, c)

    def at_x(q):
        return (y, q, z, c)

    def at_z(q):
        return (y, x, q, c)

    partner = (y, x, z, 1 - c)
    peers = [at_y((y + d) % 4) for d in range(1, 4)]
    peers += [at_x((x + d) % 4) for d in range(1, 4)]
    peers += [at_z((z + d) % NZ) for d in range(1, NZ)]
    peers += [partner]
    barrier = pltpu.get_barrier_semaphore()
    for peer in peers:
        pl.semaphore_signal(barrier, inc=1, device_id=peer, device_id_type=MESH)

    source = x == y
    load_m = pltpu.make_async_copy(m_hbm.at[0], mv, load.at[0])
    load_g = pltpu.make_async_copy(g_hbm.at[0], gv, load.at[1])
    load_r = pltpu.make_async_copy(r_hbm, rall.at[z, c], load.at[2])

    @pl.when(source)
    def _():
        load_r.start()

    load_m.start()
    load_g.start()

    @pl.when(source)
    def _():
        load_r.wait()

    pl.semaphore_wait(barrier, len(peers))

    to_x = [
        copy_to(rall.at[z, c], rall.at[z, c], rx_send.at[d - 1], rx_recv.at[0], at_x((x + d) % 4))
        for d in range(1, 4)
    ]

    @pl.when(source)
    def _():
        for copy in to_x:
            copy.start()

    load_m.wait()
    load_g.wait()
    for q in range(4):
        columns = slice(q * BLOCK, (q + 1) * BLOCK)
        bs[q] = mv[:, columns] + gv[:, columns].astype(f32)

    half = SHARD // 2
    up, down = at_y((y + 1) % 4), at_y((y + 3) % 4)
    after, before, across = (y + 1) % 4, (y + 3) % 4, (y + 2) % 4
    low, high = pl.ds(0, half), pl.ds(half, half)
    sums = [
        copy_to(bs.at[across, low], raw.at[0], s_send.at[0], s_recv.at[0], up),
        copy_to(bs.at[across, high], raw.at[1], s_send.at[1], s_recv.at[1], down),
        copy_to(bs.at[after, high], inn.at[1], s_send.at[2], s_recv.at[2], up),
        copy_to(bs.at[before, low], inn.at[0], s_send.at[3], s_recv.at[3], down),
    ]
    for copy in sums:
        copy.start()

    @pl.when(jnp.logical_not(source))
    def _():
        to_x[0].wait_recv()

    order = sorted(range(1, NZ), key=lambda d: abs(d - NZ // 2))
    to_z = [
        copy_to(rall.at[z, c], rall.at[z, c], rz_send.at[d - 1], rz_recv.at[d - 1], at_z((z + d) % NZ))
        for d in order
    ]
    for copy in to_z:
        copy.start()

    sums[0].wait_recv()
    comb[0] = raw[0] + bs[after, :half]
    sums.append(copy_to(comb.at[0], cin.at[0], s_send.at[4], s_recv.at[4], up))
    sums[4].start()
    sums[1].wait_recv()
    comb[1] = raw[1] + bs[before, half:]
    sums.append(copy_to(comb.at[1], cin.at[1], s_send.at[5], s_recv.at[5], down))
    sums[5].start()

    for copy in to_z:
        copy.wait_recv()
    over = copy_to(rall.at[:, c], rall.at[:, c], rc_send.at[0], rc_recv.at[0], partner)
    over.start()
    for copy in sums[2:]:
        copy.wait_recv()
    s_c[:half] = bs[y, :half] + inn[0] + cin[0]
    s_c[half:] = bs[y, half:] + inn[1] + cin[1]
    over.wait_recv()
    for b in range(32):
        rc[b * OWN : (b + 1) * OWN] = rall[b // 2, b % 2]
    pall[y] = jnp.dot(s_c[...], rc[...], precision=highest, preferred_element_type=f32)

    def rows_of(q, h):
        return pall.at[q, pl.ds(half * h, half)]

    gather_ring(rows_of, y, up, down, p_send, p_recv)
    projected = pall[0] + pall[1] + pall[2] + pall[3]
    p_out[...] = projected

    along_rows = (((0,), (0,)), ((), ()))
    gram[...] = lax.dot_general(projected, projected, along_rows, precision=highest, preferred_element_type=f32)
    for g in range(8):
        part = s_c[:, g * FACTOR_ROWS : (g + 1) * FACTOR_ROWS]
        mloc[g, :FACTOR_ROWS] = lax.dot_general(
            part, projected, along_rows, precision=highest, preferred_element_type=f32
        )
        mloc[g, FACTOR_ROWS:] = gram[pl.ds(pl.multiple_of(64 * y + 8 * g, 8), 8), :]

    to_core = copy_to(mloc.at[pl.ds(4 * (1 - c), 4)], crecv, c_send.at[0], c_recv.at[0], partner)
    to_core.start()
    to_core.wait_recv()
    for q in range(4):
        mx[q] = mloc[4 * c + q] + crecv[q]
    sums_x = [
        copy_to(mx.at[(x + d) % 4], xrecv.at[d - 1], x_send.at[d - 1], x_recv.at[d - 1], at_x((x + d) % 4))
        for d in (2, 1, 3)
    ]
    for copy in sums_x:
        copy.start()
    for copy in sums_x:
        copy.wait_recv()
    mz[...] = mx[x] + xrecv[0] + xrecv[1] + xrecv[2]

    owners = [(16 * t + 9) // 10 for t in range(TILES)]
    tile = (z * TILES) // NZ
    owner = (z * TILES) % NZ < TILES
    sums_z = [
        copy_to(mz.at[pl.ds(8 * t, 8)], zrecv.at[z], z_send.at[t], z_recv.at[z], at_z(owners[t]))
        for t in range(TILES)
    ]
    for t in range(TILES):

        @pl.when(z != owners[t])
        def _():
            sums_z[t].start()

    group = 4 * c + x
    rows = pl.ds(pl.multiple_of(8 * tile, 8), 8)
    to_all = [
        copy_to(
            fin, mall.at[y, group, rows], f_send.at[d - 1], f_recv.at[tile], at_z((z + d) % NZ)
        )
        for d in order
    ]

    @pl.when(owner)
    def _():
        zrecv[z] = mz[rows, :]
        for s in range(NZ):

            @pl.when(z != s)
            def _():
                copy_to(zrecv.at[s], zrecv.at[s], z_send.at[0], z_recv.at[s], partner).wait_recv()

        total = zrecv[0]
        for s in range(1, NZ):
            total = total + zrecv[s]
        fin[...] = total
        for copy in to_all:
            copy.start()
        mall[y, group, rows] = total

    for t in range(TILES):

        @pl.when(z != owners[t])
        def _():
            copy_to(
                fin, mall.at[y, group, pl.ds(8 * t, 8)], f_send.at[0], f_recv.at[t], partner
            ).wait_recv()

    east, west = at_x((x + 1) % 4), at_x((x + 3) % 4)

    @pl.when(c == 0)
    def _():
        gather_ring(lambda q, h: mall.at[y, q, pl.ds(40 * h, 40)], x, east, west, a_send, a_recv)
        gather_ring(lambda q, h: mall.at[q, pl.ds(2 * h, 2)], y, up, down, b_send, b_recv)

    @pl.when(c == 1)
    def _():
        gather_ring(lambda q, h: mall.at[q, 4 + x, pl.ds(40 * h, 40)], y, up, down, a_send, a_recv)
        gather_ring(lambda q, h: mall.at[pl.ds(2 * h, 2), 4 + q], x, east, west, b_send, b_recv)

    halves = copy_to(
        mall.at[:, pl.ds(4 * c, 4)], mall.at[:, pl.ds(4 * c, 4)], d_send.at[0], d_recv.at[0], partner
    )
    halves.start()

    @pl.when(source)
    def _():
        for copy in to_x:
            copy.wait_send()

    for copy in to_z + sums + [over, to_core] + sums_x:
        copy.wait_send()
    for t in range(TILES):

        @pl.when(z != owners[t])
        def _():
            sums_z[t].wait_send()

    @pl.when(owner)
    def _():
        for copy in to_all:
            copy.wait_send()

    halves.wait_send()
    halves.wait_recv()


def exchange(momentum, gradient, right_factor):
    sem = pltpu.SemaphoreType.DMA
    half = SHARD // 2
    counts = (3, 6, 6, 3, 1, 15, 15, 1, 1, 6, 6, 1, 1, 3, 3, TILES, NZ, 15, TILES, 6, 6, 6, 6, 1, 1)
    return pl.pallas_call(
        exchange_kernel,
        name="exchange",
        out_shape=(
            jax.ShapeDtypeStruct((SHARD, RANK), f32),
            jax.ShapeDtypeStruct((4, 8, PIECE, RANK), f32),
        ),
        in_specs=[pl.BlockSpec(memory_space=pl.ANY)] * 3,
        out_specs=(pl.BlockSpec(memory_space=VMEM),) * 2,
        scratch_shapes=[
            VMEM((SHARD, COLS), f32),
            VMEM((SHARD, COLS), jnp.bfloat16),
            VMEM((4, SHARD, BLOCK), f32),
            VMEM((2, half, BLOCK), f32),
            VMEM((2, half, BLOCK), f32),
            VMEM((2, half, BLOCK), f32),
            VMEM((2, half, BLOCK), f32),
            VMEM((SHARD, BLOCK), f32),
            VMEM((NZ, 2, OWN, RANK), f32),
            VMEM((BLOCK, RANK), f32),
            VMEM((4, SHARD, RANK), f32),
            VMEM((RANK, RANK), f32),
            VMEM((8, PIECE, RANK), f32),
            VMEM((4, PIECE, RANK), f32),
            VMEM((4, PIECE, RANK), f32),
            VMEM((3, PIECE, RANK), f32),
            VMEM((PIECE, RANK), f32),
            VMEM((NZ, 8, RANK), f32),
            VMEM((8, RANK), f32),
        ]
        + [sem((n,)) for n in counts],
        compiler_params=pltpu.CompilerParams(
            collective_id=0, has_side_effects=True, vmem_limit_bytes=40 * 1024 * 1024
        ),
    )(momentum, gradient, right_factor)


def dot(a, b, contract, precise=True):
    if not precise:
        a, b = a.astype(jnp.bfloat16), b.astype(jnp.bfloat16)
    return lax.dot_general(
        a, b, (contract, ((), ())), precision=highest if precise else None, preferred_element_type=f32
    )


def finish_kernel(m_hbm, g_hbm, p_ref, mall, new_m, update, new_f, mv, gv, a_ref, x_ref, w_ref, fbuf, load):
    load_m = pltpu.make_async_copy(m_hbm.at[0], mv, load.at[0])
    load_g = pltpu.make_async_copy(g_hbm.at[0], gv, load.at[1])
    load_m.start()
    load_g.start()
    x, z, c = (lax.axis_index(name) for name in FSDP)

    for g in range(4):
        for i in range(8):
            a_ref[64 * g + 8 * i : 64 * g + 8 * i + 8, :] = mall[g, i, FACTOR_ROWS:]
    row = lax.broadcasted_iota(jnp.int32, (RANK, RANK), 0)
    col = lax.broadcasted_iota(jnp.int32, (RANK, RANK), 1)
    gram = a_ref[...]
    diagonal = jnp.where(row == col, gram, 0.0)
    by_row = lax.rsqrt(jnp.sum(diagonal, axis=1, keepdims=True))
    by_col = lax.rsqrt(jnp.sum(diagonal, axis=0, keepdims=True))
    scaled = gram * by_row * by_col
    a_ref[...] = scaled
    bound = jnp.max(jnp.sum(jnp.abs(scaled), axis=0, keepdims=True), axis=1, keepdims=True)
    x_ref[...] = jnp.where(row == col, lax.rsqrt(bound / 1.5), 0.0)

    def step(precise):
        def body(state):
            _, count = state
            inverse = x_ref[...]
            error = dot(dot(inverse, a_ref[...], ((1,), (0,)), precise), inverse, ((1,), (1,)), precise)
            error = jnp.where(row == col, error - 1.0, error)
            lower = jnp.where(row > col, error, jnp.where(row == col, 0.5 * error, 0.0))
            x_ref[...] = inverse - dot(lower, inverse, ((1,), (0,)), precise)
            return jnp.sum(error * error), count + 1

        return body

    rough = lax.while_loop(
        lambda s: (s[0] > 0.04) & (s[1] < 12), step(False), (jnp.float32(1e9), jnp.int32(0))
    )
    del rough
    size, _ = lax.while_loop(
        lambda s: (s[0] > 1e-6) & (s[1] < 40), step(True), (jnp.float32(1e9), jnp.int32(0))
    )

    @pl.when(jnp.logical_not(size <= 1e-6))
    def _():
        w_ref[...] = a_ref[...]
        x_ref[...] = jnp.where(row == col, 1.0, 0.0)

        def eliminate(j, carry):
            work = w_ref[...]
            inverse = x_ref[...]
            column = jnp.sum(jnp.where(col == j, work, 0.0), axis=1, keepdims=True)
            line = jnp.sum(jnp.where(row == j, work, 0.0), axis=0, keepdims=True)
            own = jnp.sum(jnp.where(row == j, inverse, 0.0), axis=0, keepdims=True)
            pivot = jnp.max(jnp.where(row[:, :1] == j, column, -jnp.inf), axis=0, keepdims=True)
            ratio = jnp.where(row[:, :1] > j, column / pivot, 0.0)
            w_ref[...] = work - ratio * line
            x_ref[...] = jnp.where(row == j, own / jnp.sqrt(pivot), inverse - ratio * own)
            return carry

        lax.fori_loop(0, RANK, eliminate, 0)

    inverse = jnp.where(row >= col, x_ref[...], 0.0) * by_col
    x_ref[...] = inverse
    squares = jnp.zeros((1, RANK), f32)
    for q in range(4):
        block = mall[q, :, :FACTOR_ROWS].reshape(BLOCK, RANK)
        factor = dot(block, inverse, ((1,), (1,))) * (1.0 / REPLICAS)
        fbuf[q * BLOCK : (q + 1) * BLOCK] = factor
        squares = squares + jnp.sum(factor * factor, axis=0, keepdims=True)
    norms = jnp.sqrt(squares + epsilon)
    orthonormal = dot(p_ref[...], inverse, ((1,), (1,)))
    directions = orthonormal / norms * math.sqrt(ROWS * COLS / RANK)

    place = x * 32 + z * 2 + c
    for j in range(4):

        @pl.when(place % 4 == j)
        def _():
            own = mall[place // 32, (place % 32) // 4, OWN * j : OWN * (j + 1)]
            new_f[...] = dot(own, inverse, ((1,), (1,))) * (1.0 / REPLICAS) / norms

    load_m.wait()
    load_g.wait()
    width = 256
    for j in range(COLS // width):
        columns = slice(j * width, (j + 1) * width)
        factor = fbuf[columns, :]
        correction = dot(orthonormal, factor, ((1,), (1,)))
        new_m[0, :, columns] = mv[:, columns] + gv[:, columns].astype(f32) - (1.0 - decay_rate) * correction
        update[:, columns] = dot(directions, factor, ((1,), (1,))).astype(jnp.bfloat16)


def finish(momentum, gradient, projected, mall):
    vmem = pl.BlockSpec(memory_space=VMEM)
    anywhere = pl.BlockSpec(memory_space=pl.ANY)
    return pl.pallas_call(
        finish_kernel,
        name="finish",
        out_shape=(
            jax.ShapeDtypeStruct((1, SHARD, COLS), f32),
            jax.ShapeDtypeStruct((SHARD, COLS), jnp.bfloat16),
            jax.ShapeDtypeStruct((OWN, RANK), f32),
        ),
        in_specs=[anywhere, anywhere, vmem, vmem],
        out_specs=(vmem,) * 3,
        scratch_shapes=[
            VMEM((SHARD, COLS), f32),
            VMEM((SHARD, COLS), jnp.bfloat16),
            VMEM((RANK, RANK), f32),
            VMEM((RANK, RANK), f32),
            VMEM((RANK, RANK), f32),
            VMEM((COLS, RANK), f32),
            pltpu.SemaphoreType.DMA((2,)),
        ],
        compiler_params=pltpu.CompilerParams(vmem_limit_bytes=40 * 1024 * 1024),
    )(momentum, gradient, projected, mall)


def shards(momentum, gradient, right_factor):
    projected, mall = exchange(momentum, gradient, right_factor)
    return finish(momentum, gradient, projected, mall)


def solution(mesh):
    split = Mesh(mesh.devices.reshape(mesh.shape["rep"], NX, NZ, 2), ("rep",) + FSDP)
    in_specs = (P("rep", FSDP, None), P("rep", FSDP, None), P(FSDP, None))
    out_specs = (P("rep", FSDP, None), P(FSDP, None), P(FSDP, None))
    return jax.shard_map(
        shards, mesh=split, in_specs=in_specs, out_specs=out_specs, check_vma=False
    )
```

time: 519 us -> 114 us (0.22)
  blocking collectives: 283 us -> 0 us
  waiting for transfers between devices: 124 us -> 0 us
  Pallas kernels: 0 us -> 109 us
  other arithmetic: 55.3 us -> 0 us
  local copies, waits for them, and re-layouts: 21.4 us -> 3.14 us
  matrix products: 17.6 us -> 0 us
  starting transfers between devices: 14 us -> 0 us
    all_to_all x9 -> x0, blocking collectives: 283 us -> none  [the longest x5 132 us: sent_to_all(): lax.all_to_all(jnp.broadcast_to(shard[None], (devices, *shard.shape)), ax...]
    all_to_all x2 -> x0, waiting for transfers between devices: 124 us -> none  [sent_to_all(): lax.all_to_all(jnp.broadcast_to(shard[None], (devices, *shard.shape)), ax...]
    pallas_call x0 -> x2, Pallas kernels: none -> 109 us  [the longest x1 94.2 us: exchange(): pl.pallas_call(exchange_kernel, name='exchange', out_shape=(jax.ShapeDtyp...]
    another operation x9 -> x0, other arithmetic: 53.9 us -> none  [the longest x6 33.9 us: shards(): lower_factor = jnp.linalg.cholesky(gram_matrix)]
    dot_general x5 -> x0, matrix products: 16.4 us -> none  [the longest x1 5.27 us: shards(): lax.dot_general(columns, orthonormal, (((0,), (0,)), ((), ())), precision...]
    all_to_all x2 -> x0, starting transfers between devices: 14 us -> none  [sent_to_all(): lax.all_to_all(jnp.broadcast_to(shard[None], (devices, *shard.shape)), ax...]
    another operation x14 -> x0, local copies, waits for them, and re-layouts: 9.85 us -> none
  transfers between devices with their start and end apart: 2 -> 0, of which waited for: 2 -> 0; matrix products, arithmetic and copies ran while one was open for 0% -> 0% of each run, Pallas kernels for 0% -> 0%
where the time goes in v1:
time: 114 us; the launch traced here: 113 us
  Pallas kernels  109 us (96%)
  local copies, waits for them, and re-layouts  3.14 us (3%)
    pallas_call x1, Pallas kernels, exchange(): pl.pallas_call(exchange_kernel, name='exchange', out_shape=(jax.ShapeDtyp...  94.2 us
    pallas_call x1, Pallas kernels, finish(): pl.pallas_call(finish_kernel, name='finish', out_shape=(jax.ShapeDtypeStr...  15.2 us
    unnamed x6, local copies, waits for them, and re-layouts  3.14 us

profile of v1, /device:TPU:1, one launch (start us, length us, event | category | flops | bytes accessed | tf_op | source)
XLA Modules:
  0.0 113.2 jit_solution(8516564026082993283)
XLA Ops:
  0.6 0.0 copy-start
  0.6 1.3 %copy-done = f32[1,144,2304]{2,1,0:T(8,128)S(1)} copy-done((f32[1,144,2304]{2,1,0:T(8,128)S(1)}, f32[1,144,2304]{2,1,0:T(8,128)}, u32[]{:S(2)}) %copy-start) | copy-done | bytes 1327128
  2.0 0.0 copy-start.1
  2.0 1.1 copy-done.1
  3.0 0.0 copy-start.2
  3.0 0.7 copy-done.2
  3.8 94.2 %exchange.1 = (f32[144,256]{1,0:T(8,128)S(1)}, f32[4,8,80,256]{3,2,1,0:T(8,128)S(1)}) custom-call(f32[1,144,2304]{2,1,0:T(8,128)S(1)} %copy-done, bf16[1,144,2304]{2,1,0:T(8,128)(2,1)S(1)} %copy-done.1, f32[18,256]{1,0:T(8,128)S(1)} %copy-done.2), custom_call_target="tpu_custom_call" | custom-call | tf_op jit(solution)/shard_map/exchange/pallas_call | solution.py:296
  98.0 15.2 %finish.1 = (f32[1,144,2304]{2,1,0:T(8,128)}, bf16[144,2304]{1,0:T(8,128)(2,1)}, f32[18,256]{1,0:T(8,128)}) custom-call(f32[1,144,2304]{2,1,0:T(8,128)S(1)} %copy-done, bf16[1,144,2304]{2,1,0:T(8,128)(2,1)S(1)} %copy-done.1, f32[144,256]{1,0:T(8,128)S(1)} %get-tuple-element.5.p_ref, f32[4,8,80,256]{3,2,1,0:T(8,128)S(1)} %get-tuple-element.6.mall), custom_call_target="tpu_custom_call" | custom-call | tf_op jit(solution)/shard_map/finish/pallas_call | solution.py:435
Async XLA Ops:
  0.6 1.3 %copy-start = (f32[1,144,2304]{2,1,0:T(8,128)S(1)}, f32[1,144,2304]{2,1,0:T(8,128)}, u32[]{:S(2)}) copy-start(f32[1,144,2304]{2,1,0:T(8,128)} %m_hbm.3) | copy-start | bytes 3981316
  2.0 1.1 copy-start.1
  3.0 0.7 copy-start.2

commit v2 on v1

--- a/solution.py
+++ b/solution.py
@@ -65,8 +65,8 @@
 
 
 def exchange_kernel(
-    m_hbm, g_hbm, r_hbm, p_out, mall,
-    mv, gv, bs, raw, comb, cin, inn, s_c, rall, rc, pall, gram, mloc, crecv, mx, xrecv, mz, zrecv, fin,
+    m_hbm, g_hbm, r_hbm, buffer, p_out, mall,
+    mv, gv, bs, raw, comb, cin, inn, s_c, s_t, rall, rc, pall, gram, mloc, crecv, mx, xrecv, mz, zrecv, fin,
     load, s_send, s_recv, rx_send, rx_recv, rz_send, rz_recv, rc_send, rc_recv, p_send, p_recv,
     c_send, c_recv, x_send, x_recv, z_send, z_recv, f_send, f_recv, a_send, a_recv, b_send, b_recv,
     d_send, d_recv,
@@ -83,14 +83,10 @@
         return (y, x, q, c)
 
     partner = (y, x, z, 1 - c)
-    peers = [at_y((y + d) % 4) for d in range(1, 4)]
+    peers = [at_z((z + d) % NZ) for d in sorted(range(1, NZ), key=lambda d: abs(d - NZ // 2))]
+    peers += [at_y((y + d) % 4) for d in range(1, 4)]
     peers += [at_x((x + d) % 4) for d in range(1, 4)]
-    peers += [at_z((z + d) % NZ) for d in range(1, NZ)]
     peers += [partner]
-    barrier = pltpu.get_barrier_semaphore()
-    for peer in peers:
-        pl.semaphore_signal(barrier, inc=1, device_id=peer, device_id_type=MESH)
-
     source = x == y
     load_m = pltpu.make_async_copy(m_hbm.at[0], mv, load.at[0])
     load_g = pltpu.make_async_copy(g_hbm.at[0], gv, load.at[1])
@@ -102,6 +98,17 @@
 
     load_m.start()
     load_g.start()
+    barrier = pltpu.get_barrier_semaphore()
+    for peer in peers:
+        pl.semaphore_signal(barrier, inc=1, device_id=peer, device_id_type=MESH)
+
+    load_m.wait()
+    load_g.wait()
+    for q in range(4):
+        columns = slice(q * BLOCK, (q + 1) * BLOCK)
+        part = mv[:, columns] + gv[:, columns].astype(f32)
+        buffer[:, columns] = part
+        bs[q] = part
 
     @pl.when(source)
     def _():
@@ -118,12 +125,6 @@
     def _():
         for copy in to_x:
             copy.start()
-
-    load_m.wait()
-    load_g.wait()
-    for q in range(4):
-        columns = slice(q * BLOCK, (q + 1) * BLOCK)
-        bs[q] = mv[:, columns] + gv[:, columns].astype(f32)
 
     half = SHARD // 2
     up, down = at_y((y + 1) % 4), at_y((y + 3) % 4)
@@ -142,11 +143,11 @@
     def _():
         to_x[0].wait_recv()
 
-    order = sorted(range(1, NZ), key=lambda d: abs(d - NZ // 2))
-    to_z = [
-        copy_to(rall.at[z, c], rall.at[z, c], rz_send.at[d - 1], rz_recv.at[d - 1], at_z((z + d) % NZ))
-        for d in order
-    ]
+    def along_z(owner, far, step):
+        block = rall.at[(z + NZ - owner) % NZ, c]
+        return copy_to(block, block, rz_send.at[far % NZ - 1], rz_recv.at[far % NZ - 1], at_z((z + NZ + step) % NZ))
+
+    to_z = [along_z(0, d, d) for d in (4, -4, 3, -3, 2, -2, 1, -1)]
     for copy in to_z:
         copy.start()
 
@@ -159,14 +160,25 @@
     sums.append(copy_to(comb.at[1], cin.at[1], s_send.at[5], s_recv.at[5], down))
     sums[5].start()
 
-    for copy in to_z:
-        copy.wait_recv()
-    over = copy_to(rall.at[:, c], rall.at[:, c], rc_send.at[0], rc_recv.at[0], partner)
-    over.start()
+    to_z[0].wait_recv()
+    beyond = [along_z(4, 4 + d, d) for d in (4, 3, 2, 1)]
+    for copy in beyond:
+        copy.start()
+    to_z[1].wait_recv()
+    beyond += [along_z(-4, -4 - d, -d) for d in (3, 2, 1)]
+    for copy in beyond[4:]:
+        copy.start()
+
     for copy in sums[2:]:
         copy.wait_recv()
     s_c[:half] = bs[y, :half] + inn[0] + cin[0]
     s_c[half:] = bs[y, half:] + inn[1] + cin[1]
+    s_t[...] = s_c[...].T
+
+    for copy in to_z[2:] + beyond:
+        copy.wait_recv()
+    over = copy_to(rall.at[:, c], rall.at[:, c], rc_send.at[0], rc_recv.at[0], partner)
+    over.start()
     over.wait_recv()
     for b in range(32):
         rc[b * OWN : (b + 1) * OWN] = rall[b // 2, b % 2]
@@ -181,24 +193,30 @@
 
     along_rows = (((0,), (0,)), ((), ()))
     gram[...] = lax.dot_general(projected, projected, along_rows, precision=highest, preferred_element_type=f32)
-    for g in range(8):
-        part = s_c[:, g * FACTOR_ROWS : (g + 1) * FACTOR_ROWS]
-        mloc[g, :FACTOR_ROWS] = lax.dot_general(
-            part, projected, along_rows, precision=highest, preferred_element_type=f32
-        )
-        mloc[g, FACTOR_ROWS:] = gram[pl.ds(pl.multiple_of(64 * y + 8 * g, 8), 8), :]
-
+
+    def fill(side):
+        rows = pl.ds(pl.multiple_of(4 * FACTOR_ROWS * side, 8), 4 * FACTOR_ROWS)
+        part = jnp.dot(s_t[rows, :], projected, precision=highest, preferred_element_type=f32)
+        for i in range(4):
+            mloc[4 * side + i, :FACTOR_ROWS] = part[i * FACTOR_ROWS : (i + 1) * FACTOR_ROWS]
+            mloc[4 * side + i, FACTOR_ROWS:] = gram[
+                pl.ds(pl.multiple_of(64 * y + 8 * (4 * side + i), 8), 8), :
+            ]
+
+    fill(1 - c)
     to_core = copy_to(mloc.at[pl.ds(4 * (1 - c), 4)], crecv, c_send.at[0], c_recv.at[0], partner)
     to_core.start()
+    fill(c)
     to_core.wait_recv()
-    for q in range(4):
-        mx[q] = mloc[4 * c + q] + crecv[q]
     sums_x = [
         copy_to(mx.at[(x + d) % 4], xrecv.at[d - 1], x_send.at[d - 1], x_recv.at[d - 1], at_x((x + d) % 4))
         for d in (2, 1, 3)
     ]
-    for copy in sums_x:
-        copy.start()
+    for d, copy in zip((2, 1, 3), sums_x, strict=True):
+        q = (x + d) % 4
+        mx[q] = mloc[4 * c + q] + crecv[q]
+        copy.start()
+    mx[x] = mloc[4 * c + x] + crecv[x]
     for copy in sums_x:
         copy.wait_recv()
     mz[...] = mx[x] + xrecv[0] + xrecv[1] + xrecv[2]
@@ -222,7 +240,7 @@
         copy_to(
             fin, mall.at[y, group, rows], f_send.at[d - 1], f_recv.at[tile], at_z((z + d) % NZ)
         )
-        for d in order
+        for d in sorted(range(1, NZ), key=lambda d: abs(d - NZ // 2))
     ]
 
     @pl.when(owner)
@@ -250,29 +268,93 @@
                 fin, mall.at[y, group, pl.ds(8 * t, 8)], f_send.at[0], f_recv.at[t], partner
             ).wait_recv()
 
-    east, west = at_x((x + 1) % 4), at_x((x + 3) % 4)
-
-    @pl.when(c == 0)
-    def _():
-        gather_ring(lambda q, h: mall.at[y, q, pl.ds(40 * h, 40)], x, east, west, a_send, a_recv)
-        gather_ring(lambda q, h: mall.at[q, pl.ds(2 * h, 2)], y, up, down, b_send, b_recv)
-
-    @pl.when(c == 1)
-    def _():
-        gather_ring(lambda q, h: mall.at[q, 4 + x, pl.ds(40 * h, 40)], y, up, down, a_send, a_recv)
-        gather_ring(lambda q, h: mall.at[pl.ds(2 * h, 2), 4 + q], x, east, west, b_send, b_recv)
-
-    halves = copy_to(
-        mall.at[:, pl.ds(4 * c, 4)], mall.at[:, pl.ds(4 * c, 4)], d_send.at[0], d_recv.at[0], partner
-    )
-    halves.start()
+    first, second = x * (1 - c) + y * c, y * (1 - c) + x * c
+
+    def turned(a, b):
+        return (b * (1 - c) + a * c, a * (1 - c) + b * c)
+
+    def block_of(k, j):
+        at, to = turned((first + k) % 4, (second + j) % 4)
+        return mall.at[at, 4 * c + to]
+
+    def half_of(k, j, h):
+        at, to = turned((first + k) % 4, (second + j) % 4)
+        return mall.at[at, 4 * c + to, pl.ds(h * (PIECE // 2), PIECE // 2)]
+
+    def on_first(k, h, step, i):
+        device = turned((first + step) % 4, second) + (z, c)
+        return copy_to(half_of(k, 0, h), half_of(k, 0, h), a_send.at[i], a_recv.at[i], device)
+
+    def on_second(k, j, h, step, i):
+        device = turned(first, (second + step) % 4) + (z, c)
+        i = 6 * k + i
+        return copy_to(half_of(k, j, h), half_of(k, j, h), b_send.at[i], b_recv.at[i], device)
+
+    def on_chip(k, j):
+        i = 4 * k + j
+        return copy_to(block_of(k, j), block_of(k, j), d_send.at[i], d_recv.at[i], partner)
+
+    ring = [on_first(0, 0, 1, 0), on_first(0, 1, 3, 1), on_first(0, 1, 1, 2), on_first(0, 0, 3, 3)]
+    ring += [on_first(3, 0, 1, 4), on_first(1, 1, 3, 5)]
+    across_ring = [
+        [on_second(k, 0, 0, 1, 0), on_second(k, 0, 1, 3, 1), on_second(k, 0, 1, 1, 2)]
+        + [on_second(k, 0, 0, 3, 3), on_second(k, 3, 0, 1, 4), on_second(k, 1, 1, 3, 5)]
+        for k in range(4)
+    ]
+    cores = [[on_chip(k, j) for j in range(4)] for k in range(4)]
+
+    def start_half(k, h):
+        for i in ((0, 3), (1, 2))[h]:
+            across_ring[k][i].start()
+
+    def hand_on(k):
+        for i in range(2):
+            across_ring[k][i].wait_recv()
+            across_ring[k][4 + i].start()
+
+    def complete(k):
+        for i in range(2, 6):
+            across_ring[k][i].wait_recv()
+        for j in range(1, 4):
+            cores[k][j].start()
+
+    for copy in ring[:4]:
+        copy.start()
+    start_half(0, 0)
+    start_half(0, 1)
+    cores[0][0].start()
+    ring[0].wait_recv()
+    ring[4].start()
+    start_half(3, 0)
+    ring[1].wait_recv()
+    ring[5].start()
+    start_half(1, 1)
+    ring[2].wait_recv()
+    start_half(3, 1)
+    ring[3].wait_recv()
+    start_half(1, 0)
+    cores[3][0].start()
+    cores[1][0].start()
+    hand_on(0)
+    ring[4].wait_recv()
+    start_half(2, 0)
+    ring[5].wait_recv()
+    start_half(2, 1)
+    cores[2][0].start()
+    hand_on(3)
+    hand_on(1)
+    complete(0)
+    hand_on(2)
+    complete(3)
+    complete(1)
+    complete(2)
 
     @pl.when(source)
     def _():
         for copy in to_x:
             copy.wait_send()
 
-    for copy in to_z + sums + [over, to_core] + sums_x:
+    for copy in to_z + beyond + sums + [over, to_core] + sums_x + ring:
         copy.wait_send()
     for t in range(TILES):
 
@@ -285,23 +367,28 @@
         for copy in to_all:
             copy.wait_send()
 
-    halves.wait_send()
-    halves.wait_recv()
+    for k in range(4):
+        for copy in across_ring[k] + cores[k]:
+            copy.wait_send()
+    for k in range(4):
+        for copy in cores[k]:
+            copy.wait_recv()
 
 
 def exchange(momentum, gradient, right_factor):
     sem = pltpu.SemaphoreType.DMA
     half = SHARD // 2
-    counts = (3, 6, 6, 3, 1, 15, 15, 1, 1, 6, 6, 1, 1, 3, 3, TILES, NZ, 15, TILES, 6, 6, 6, 6, 1, 1)
+    counts = (3, 6, 6, 3, 1, 15, 15, 1, 1, 6, 6, 1, 1, 3, 3, TILES, NZ, 15, TILES, 6, 6, 24, 24, 16, 16)
     return pl.pallas_call(
         exchange_kernel,
         name="exchange",
         out_shape=(
+            jax.ShapeDtypeStruct((SHARD, COLS), f32),
             jax.ShapeDtypeStruct((SHARD, RANK), f32),
             jax.ShapeDtypeStruct((4, 8, PIECE, RANK), f32),
         ),
-        in_specs=[pl.BlockSpec(memory_space=pl.ANY)] * 3,
-        out_specs=(pl.BlockSpec(memory_space=VMEM),) * 2,
+        in_specs=[pl.BlockSpec(memory_space=pltpu.HBM)] * 3,
+        out_specs=(pl.BlockSpec(memory_space=VMEM),) * 3,
         scratch_shapes=[
             VMEM((SHARD, COLS), f32),
             VMEM((SHARD, COLS), jnp.bfloat16),
@@ -311,6 +398,7 @@
             VMEM((2, half, BLOCK), f32),
             VMEM((2, half, BLOCK), f32),
             VMEM((SHARD, BLOCK), f32),
+            VMEM((BLOCK, SHARD), f32),
             VMEM((NZ, 2, OWN, RANK), f32),
             VMEM((BLOCK, RANK), f32),
             VMEM((4, SHARD, RANK), f32),
@@ -327,7 +415,7 @@
         compiler_params=pltpu.CompilerParams(
             collective_id=0, has_side_effects=True, vmem_limit_bytes=40 * 1024 * 1024
         ),
-    )(momentum, gradient, right_factor)
+    )(*(pltpu.with_memory_space_constraint(a, pltpu.HBM) for a in (momentum, gradient, right_factor)))
 
 
 def dot(a, b, contract, precise=True):
@@ -338,11 +426,24 @@
     )
 
 
-def finish_kernel(m_hbm, g_hbm, p_ref, mall, new_m, update, new_f, mv, gv, a_ref, x_ref, w_ref, fbuf, load):
-    load_m = pltpu.make_async_copy(m_hbm.at[0], mv, load.at[0])
-    load_g = pltpu.make_async_copy(g_hbm.at[0], gv, load.at[1])
-    load_m.start()
-    load_g.start()
+def split(a):
+    top = a.astype(jnp.bfloat16)
+    return top, (a - top.astype(f32)).astype(jnp.bfloat16)
+
+
+def dot_split(a, b):
+    (a_top, a_rest), (b_top, b_rest) = a, b
+    turn = (((1,), (1,)), ((), ()))
+
+    def product(left, right):
+        return lax.dot_general(left, right, turn, preferred_element_type=f32)
+
+    return product(a_top, b_top) + (product(a_top, b_rest) + product(a_rest, b_top))
+
+
+def finish_kernel(
+    buffer, p_ref, mall, new_m, update, new_f, a_ref, x_ref, w_ref, top_ref, rest_ref, m_buf, u_buf, m_sem, u_sem
+):
     x, z, c = (lax.axis_index(name) for name in FSDP)
 
     for g in range(4):
@@ -400,11 +501,14 @@
 
     inverse = jnp.where(row >= col, x_ref[...], 0.0) * by_col
     x_ref[...] = inverse
+    halves = split(inverse)
     squares = jnp.zeros((1, RANK), f32)
     for q in range(4):
         block = mall[q, :, :FACTOR_ROWS].reshape(BLOCK, RANK)
-        factor = dot(block, inverse, ((1,), (1,))) * (1.0 / REPLICAS)
-        fbuf[q * BLOCK : (q + 1) * BLOCK] = factor
+        factor = dot_split(split(block), halves) * (1.0 / REPLICAS)
+        top, rest = split(factor)
+        top_ref[q * BLOCK : (q + 1) * BLOCK] = top
+        rest_ref[q * BLOCK : (q + 1) * BLOCK] = rest
         squares = squares + jnp.sum(factor * factor, axis=0, keepdims=True)
     norms = jnp.sqrt(squares + epsilon)
     orthonormal = dot(p_ref[...], inverse, ((1,), (1,)))
@@ -418,20 +522,26 @@
             own = mall[place // 32, (place % 32) // 4, OWN * j : OWN * (j + 1)]
             new_f[...] = dot(own, inverse, ((1,), (1,))) * (1.0 / REPLICAS) / norms
 
-    load_m.wait()
-    load_g.wait()
+    both = split(jnp.concatenate([orthonormal, directions], axis=0))
     width = 256
+    copies = []
     for j in range(COLS // width):
         columns = slice(j * width, (j + 1) * width)
-        factor = fbuf[columns, :]
-        correction = dot(orthonormal, factor, ((1,), (1,)))
-        new_m[0, :, columns] = mv[:, columns] + gv[:, columns].astype(f32) - (1.0 - decay_rate) * correction
-        update[:, columns] = dot(directions, factor, ((1,), (1,))).astype(jnp.bfloat16)
-
-
-def finish(momentum, gradient, projected, mall):
+        products = dot_split(both, (top_ref[columns, :], rest_ref[columns, :]))
+        m_buf[:, columns] = buffer[:, columns] - (1.0 - decay_rate) * products[:SHARD]
+        u_buf[:, columns] = products[SHARD:].astype(jnp.bfloat16)
+        part = pl.ds(j * width, width)
+        copies.append(pltpu.make_async_copy(m_buf.at[:, part], new_m.at[0, :, part], m_sem.at[j]))
+        copies.append(pltpu.make_async_copy(u_buf.at[:, part], update.at[:, part], u_sem.at[j]))
+        copies[-2].start()
+        copies[-1].start()
+    for copy in copies:
+        copy.wait()
+
+
+def finish(buffer, projected, mall):
     vmem = pl.BlockSpec(memory_space=VMEM)
-    anywhere = pl.BlockSpec(memory_space=pl.ANY)
+    anywhere = pl.BlockSpec(memory_space=pltpu.HBM)
     return pl.pallas_call(
         finish_kernel,
         name="finish",
@@ -440,24 +550,25 @@
             jax.ShapeDtypeStruct((SHARD, COLS), jnp.bfloat16),
             jax.ShapeDtypeStruct((OWN, RANK), f32),
         ),
-        in_specs=[anywhere, anywhere, vmem, vmem],
-        out_specs=(vmem,) * 3,
+        in_specs=[vmem] * 3,
+        out_specs=(anywhere, anywhere, vmem),
         scratch_shapes=[
-            VMEM((SHARD, COLS), f32),
-            VMEM((SHARD, COLS), jnp.bfloat16),
             VMEM((RANK, RANK), f32),
             VMEM((RANK, RANK), f32),
             VMEM((RANK, RANK), f32),
-            VMEM((COLS, RANK), f32),
-            pltpu.SemaphoreType.DMA((2,)),
+            VMEM((COLS, RANK), jnp.bfloat16),
+            VMEM((COLS, RANK), jnp.bfloat16),
+            VMEM((SHARD, COLS), f32),
+            VMEM((SHARD, COLS), jnp.bfloat16),
+            pltpu.SemaphoreType.DMA((9,)),
+            pltpu.SemaphoreType.DMA((9,)),
         ],
         compiler_params=pltpu.CompilerParams(vmem_limit_bytes=40 * 1024 * 1024),
-    )(momentum, gradient, projected, mall)
+    )(buffer, projected, mall)
 
 
 def shards(momentum, gradient, right_factor):
-    projected, mall = exchange(momentum, gradient, right_factor)
-    return finish(momentum, gradient, projected, mall)
+    return finish(*exchange(momentum, gradient, right_factor))
 
 
 def solution(mesh):

time: 114 us -> 95.2 us (0.84)
  Pallas kernels: 109 us -> 94.2 us
  local copies, waits for them, and re-layouts: 3.14 us -> 0 us
    pallas_call x1, Pallas kernels: 94.2 us -> 83.7 us  [exchange(): pl.pallas_call(exchange_kernel, name='exchange', out_shape=(jax.ShapeDtyp...]
    pallas_call x1, Pallas kernels: 15.2 us -> 10.6 us  [finish(): pl.pallas_call(finish_kernel, name='finish', out_shape=(jax.ShapeDtypeStr...]
    unnamed x6 -> x0, local copies, waits for them, and re-layouts: 3.14 us -> none
where the time goes in v2:
time: 95.2 us; the launch traced here: 94.9 us
  Pallas kernels  94.2 us (99%)
    pallas_call x1, Pallas kernels, exchange(): pl.pallas_call(exchange_kernel, name='exchange', out_shape=(jax.ShapeDtyp...  83.7 us
    pallas_call x1, Pallas kernels, finish(): pl.pallas_call(finish_kernel, name='finish', out_shape=(jax.ShapeDtypeStr...  10.6 us

profile of v2, /device:TPU:1, one launch (start us, length us, event | category | flops | bytes accessed | tf_op | source)
XLA Modules:
  0.0 94.9 jit_solution(17879002384845201615)
XLA Ops:
  0.6 83.7 %exchange.1 = (f32[144,2304]{1,0:T(8,128)S(1)}, f32[144,256]{1,0:T(8,128)S(1)}, f32[4,8,80,256]{3,2,1,0:T(8,128)S(1)}) custom-call(f32[1,144,2304]{2,1,0:T(8,128)} %m_hbm.1, bf16[1,144,2304]{2,1,0:T(8,128)(2,1)} %g_hbm.1, f32[18,256]{1,0:T(8,128)} %r_hbm.1), custom_call_target="tpu_custom_call" | custom-call | tf_op jit(solution)/shard_map/exchange/pallas_call | solution.py:382
  84.3 10.6 %finish.1 = (f32[1,144,2304]{2,1,0:T(8,128)}, bf16[144,2304]{1,0:T(8,128)(2,1)}, f32[18,256]{1,0:T(8,128)}) custom-call(f32[144,2304]{1,0:T(8,128)S(1)} %get-tuple-element.6.buffer, f32[144,256]{1,0:T(8,128)S(1)} %get-tuple-element.7.p_ref, f32[4,8,80,256]{3,2,1,0:T(8,128)S(1)} %get-tuple-element.8.mall), custom_call_target="tpu_custom_call" | custom-call | tf_op jit(solution)/shard_map/finish/pallas_call | solution.py:545

commit v3 on v2

--- a/solution.py
+++ b/solution.py
@@ -64,12 +64,47 @@
         copy.wait_send()
 
 
+def dot(a, b, contract, precise=True):
+    if not precise:
+        a, b = a.astype(jnp.bfloat16), b.astype(jnp.bfloat16)
+    return lax.dot_general(
+        a, b, (contract, ((), ())), precision=highest if precise else None, preferred_element_type=f32
+    )
+
+
+def positions():
+    shape = (RANK, RANK)
+    return lax.broadcasted_iota(jnp.int32, shape, 0), lax.broadcasted_iota(jnp.int32, shape, 1)
+
+
+def invert_start(gram, a_ref, x_ref, scale):
+    row, col = positions()
+    diagonal = jnp.where(row == col, gram, 0.0)
+    by_row = lax.rsqrt(jnp.sum(diagonal, axis=1, keepdims=True))
+    by_col = lax.rsqrt(jnp.sum(diagonal, axis=0, keepdims=True))
+    scaled = gram * by_row * by_col
+    a_ref[...] = scaled
+    scale[...] = by_col
+    bound = jnp.max(jnp.sum(jnp.abs(scaled), axis=0, keepdims=True), axis=1, keepdims=True)
+    x_ref[...] = jnp.where(row == col, lax.rsqrt(bound / 1.5), 0.0)
+
+
+def invert_step(a_ref, x_ref, precise):
+    row, col = positions()
+    inverse = x_ref[...]
+    error = dot(dot(inverse, a_ref[...], ((1,), (0,)), precise), inverse, ((1,), (1,)), precise)
+    error = jnp.where(row == col, error - 1.0, error)
+    lower = jnp.where(row > col, error, jnp.where(row == col, 0.5 * error, 0.0))
+    x_ref[...] = inverse - dot(lower, inverse, ((1,), (0,)), precise)
+    return error
+
+
 def exchange_kernel(
-    m_hbm, g_hbm, r_hbm, buffer, p_out, mall,
-    mv, gv, bs, raw, comb, cin, inn, s_c, s_t, rall, rc, pall, gram, mloc, crecv, mx, xrecv, mz, zrecv, fin,
+    m_hbm, g_hbm, r_hbm, buffer, p_out, mall, a_out, x_out, scale,
+    mv, gv, bs, raw, comb, cin, inn, s_c, s_t, rall, rc, pall, gram, mloc, crecv, mx, xrecv, mz, zrecv, fin, zall, gall,
     load, s_send, s_recv, rx_send, rx_recv, rz_send, rz_recv, rc_send, rc_recv, p_send, p_recv,
     c_send, c_recv, x_send, x_recv, z_send, z_recv, f_send, f_recv, a_send, a_recv, b_send, b_recv,
-    d_send, d_recv,
+    d_send, d_recv, gx_send, gx_recv, gy_send, gy_recv, gc_send, gc_recv,
 ):
     y, x, z, c = (lax.axis_index(name) for name in ("rep",) + FSDP)
 
@@ -83,7 +118,7 @@
         return (y, x, q, c)
 
     partner = (y, x, z, 1 - c)
-    peers = [at_z((z + d) % NZ) for d in sorted(range(1, NZ), key=lambda d: abs(d - NZ // 2))]
+    peers = [at_z((z + NZ + d) % NZ) for d in (4, -4, 3, -3, 2, -2, 1, -1)]
     peers += [at_y((y + d) % 4) for d in range(1, 4)]
     peers += [at_x((x + d) % 4) for d in range(1, 4)]
     peers += [partner]
@@ -238,7 +273,7 @@
     rows = pl.ds(pl.multiple_of(8 * tile, 8), 8)
     to_all = [
         copy_to(
-            fin, mall.at[y, group, rows], f_send.at[d - 1], f_recv.at[tile], at_z((z + d) % NZ)
+            fin, zall.at[rows], f_send.at[d - 1], f_recv.at[tile], at_z((z + d) % NZ)
         )
         for d in sorted(range(1, NZ), key=lambda d: abs(d - NZ // 2))
     ]
@@ -258,15 +293,32 @@
         fin[...] = total
         for copy in to_all:
             copy.start()
-        mall[y, group, rows] = total
-
-    for t in range(TILES):
-
+        zall[rows, :] = total
+
+    def tile_here(t):
         @pl.when(z != owners[t])
         def _():
-            copy_to(
-                fin, mall.at[y, group, pl.ds(8 * t, 8)], f_send.at[0], f_recv.at[t], partner
-            ).wait_recv()
+            copy_to(fin, zall.at[pl.ds(8 * t, 8)], f_send.at[0], f_recv.at[t], partner).wait_recv()
+
+    tile_here(TILES - 1)
+    gram_rows = pl.ds(FACTOR_ROWS, 8)
+    gram_x = [
+        copy_to(
+            zall.at[gram_rows], gall.at[y, group], gx_send.at[d - 1], gx_recv.at[d - 1], at_x((x + d) % 4)
+        )
+        for d in (2, 1, 3)
+    ]
+    mine = pl.ds(4 * c, 4)
+    gram_y = [
+        copy_to(gall.at[y, mine], gall.at[y, mine], gy_send.at[d - 1], gy_recv.at[d - 1], at_y((y + d) % 4))
+        for d in (2, 1, 3)
+    ]
+    gram_core = copy_to(gall.at[:, mine], gall.at[:, mine], gc_send.at[0], gc_recv.at[0], partner)
+    for copy in gram_x:
+        copy.start()
+    gall[y, group] = zall[gram_rows, :]
+    for t in range(TILES - 1):
+        tile_here(t)
 
     first, second = x * (1 - c) + y * c, y * (1 - c) + x * c
 
@@ -279,20 +331,24 @@
 
     def half_of(k, j, h):
         at, to = turned((first + k) % 4, (second + j) % 4)
-        return mall.at[at, 4 * c + to, pl.ds(h * (PIECE // 2), PIECE // 2)]
+        return mall.at[at, 4 * c + to, pl.ds(40 * h, 40 - 8 * h)]
+
+    def source_of(k, j, h):
+        return half_of(k, j, h) if k or j else zall.at[pl.ds(40 * h, 40 - 8 * h)]
 
     def on_first(k, h, step, i):
         device = turned((first + step) % 4, second) + (z, c)
-        return copy_to(half_of(k, 0, h), half_of(k, 0, h), a_send.at[i], a_recv.at[i], device)
+        return copy_to(source_of(k, 0, h), half_of(k, 0, h), a_send.at[i], a_recv.at[i], device)
 
     def on_second(k, j, h, step, i):
         device = turned(first, (second + step) % 4) + (z, c)
         i = 6 * k + i
-        return copy_to(half_of(k, j, h), half_of(k, j, h), b_send.at[i], b_recv.at[i], device)
+        return copy_to(source_of(k, j, h), half_of(k, j, h), b_send.at[i], b_recv.at[i], device)
 
     def on_chip(k, j):
         i = 4 * k + j
-        return copy_to(block_of(k, j), block_of(k, j), d_send.at[i], d_recv.at[i], partner)
+        source = block_of(k, j) if k or j else zall.at[pl.ds(0, FACTOR_ROWS)]
+        return copy_to(source, block_of(k, j), d_send.at[i], d_recv.at[i], partner)
 
     ring = [on_first(0, 0, 1, 0), on_first(0, 1, 3, 1), on_first(0, 1, 1, 2), on_first(0, 0, 3, 3)]
     ring += [on_first(3, 0, 1, 4), on_first(1, 1, 3, 5)]
@@ -323,6 +379,11 @@
     start_half(0, 0)
     start_half(0, 1)
     cores[0][0].start()
+    mall[y, group] = zall[:FACTOR_ROWS, :]
+    for copy in gram_x:
+        copy.wait_recv()
+    for copy in gram_y:
+        copy.start()
     ring[0].wait_recv()
     ring[4].start()
     start_half(3, 0)
@@ -335,6 +396,9 @@
     start_half(1, 0)
     cores[3][0].start()
     cores[1][0].start()
+    for copy in gram_y:
+        copy.wait_recv()
+    gram_core.start()
     hand_on(0)
     ring[4].wait_recv()
     start_half(2, 0)
@@ -343,10 +407,20 @@
     cores[2][0].start()
     hand_on(3)
     hand_on(1)
+    gram_core.wait_recv()
+    invert_start(gall[...].reshape(RANK, RANK), a_out, x_out, scale)
+    invert_step(a_out, x_out, False)
+    invert_step(a_out, x_out, False)
     complete(0)
+    invert_step(a_out, x_out, False)
     hand_on(2)
+    invert_step(a_out, x_out, False)
+    invert_step(a_out, x_out, False)
     complete(3)
+    invert_step(a_out, x_out, False)
     complete(1)
+    invert_step(a_out, x_out, False)
+    invert_step(a_out, x_out, True)
     complete(2)
 
     @pl.when(source)
@@ -354,7 +428,7 @@
         for copy in to_x:
             copy.wait_send()
 
-    for copy in to_z + beyond + sums + [over, to_core] + sums_x + ring:
+    for copy in to_z + beyond + sums + [over, to_core, gram_core] + sums_x + ring + gram_x + gram_y:
         copy.wait_send()
     for t in range(TILES):
 
@@ -378,17 +452,20 @@
 def exchange(momentum, gradient, right_factor):
     sem = pltpu.SemaphoreType.DMA
     half = SHARD // 2
-    counts = (3, 6, 6, 3, 1, 15, 15, 1, 1, 6, 6, 1, 1, 3, 3, TILES, NZ, 15, TILES, 6, 6, 24, 24, 16, 16)
+    counts = (3, 6, 6, 3, 1, 15, 15, 1, 1, 6, 6, 1, 1, 3, 3, TILES, NZ, 15, TILES, 6, 6, 24, 24, 16, 16, 3, 3, 3, 3, 1, 1)
     return pl.pallas_call(
         exchange_kernel,
         name="exchange",
         out_shape=(
             jax.ShapeDtypeStruct((SHARD, COLS), f32),
             jax.ShapeDtypeStruct((SHARD, RANK), f32),
-            jax.ShapeDtypeStruct((4, 8, PIECE, RANK), f32),
+            jax.ShapeDtypeStruct((4, 8, FACTOR_ROWS, RANK), f32),
+            jax.ShapeDtypeStruct((RANK, RANK), f32),
+            jax.ShapeDtypeStruct((RANK, RANK), f32),
+            jax.ShapeDtypeStruct((1, RANK), f32),
         ),
         in_specs=[pl.BlockSpec(memory_space=pltpu.HBM)] * 3,
-        out_specs=(pl.BlockSpec(memory_space=VMEM),) * 3,
+        out_specs=(pl.BlockSpec(memory_space=VMEM),) * 6,
         scratch_shapes=[
             VMEM((SHARD, COLS), f32),
             VMEM((SHARD, COLS), jnp.bfloat16),
@@ -410,6 +487,8 @@
             VMEM((PIECE, RANK), f32),
             VMEM((NZ, 8, RANK), f32),
             VMEM((8, RANK), f32),
+            VMEM((PIECE, RANK), f32),
+            VMEM((4, 8, 8, RANK), f32),
         ]
         + [sem((n,)) for n in counts],
         compiler_params=pltpu.CompilerParams(
@@ -418,14 +497,6 @@
     )(*(pltpu.with_memory_space_constraint(a, pltpu.HBM) for a in (momentum, gradient, right_factor)))
 
 
-def dot(a, b, contract, precise=True):
-    if not precise:
-        a, b = a.astype(jnp.bfloat16), b.astype(jnp.bfloat16)
-    return lax.dot_general(
-        a, b, (contract, ((), ())), precision=highest if precise else None, preferred_element_type=f32
-    )
-
-
 def split(a):
     top = a.astype(jnp.bfloat16)
     return top, (a - top.astype(f32)).astype(jnp.bfloat16)
@@ -442,45 +513,23 @@
 
 
 def finish_kernel(
-    buffer, p_ref, mall, new_m, update, new_f, a_ref, x_ref, w_ref, top_ref, rest_ref, m_buf, u_buf, m_sem, u_sem
+    buffer, p_ref, mall, a_ref, x_first, scale, new_m, update, new_f,
+    x_ref, w_ref, top_ref, rest_ref, m_buf, u_buf, m_sem, u_sem,
 ):
     x, z, c = (lax.axis_index(name) for name in FSDP)
 
-    for g in range(4):
-        for i in range(8):
-            a_ref[64 * g + 8 * i : 64 * g + 8 * i + 8, :] = mall[g, i, FACTOR_ROWS:]
-    row = lax.broadcasted_iota(jnp.int32, (RANK, RANK), 0)
-    col = lax.broadcasted_iota(jnp.int32, (RANK, RANK), 1)
-    gram = a_ref[...]
-    diagonal = jnp.where(row == col, gram, 0.0)
-    by_row = lax.rsqrt(jnp.sum(diagonal, axis=1, keepdims=True))
-    by_col = lax.rsqrt(jnp.sum(diagonal, axis=0, keepdims=True))
-    scaled = gram * by_row * by_col
-    a_ref[...] = scaled
-    bound = jnp.max(jnp.sum(jnp.abs(scaled), axis=0, keepdims=True), axis=1, keepdims=True)
-    x_ref[...] = jnp.where(row == col, lax.rsqrt(bound / 1.5), 0.0)
-
-    def step(precise):
-        def body(state):
-            _, count = state
-            inverse = x_ref[...]
-            error = dot(dot(inverse, a_ref[...], ((1,), (0,)), precise), inverse, ((1,), (1,)), precise)
-            error = jnp.where(row == col, error - 1.0, error)
-            lower = jnp.where(row > col, error, jnp.where(row == col, 0.5 * error, 0.0))
-            x_ref[...] = inverse - dot(lower, inverse, ((1,), (0,)), precise)
-            return jnp.sum(error * error), count + 1
-
-        return body
-
-    rough = lax.while_loop(
-        lambda s: (s[0] > 0.04) & (s[1] < 12), step(False), (jnp.float32(1e9), jnp.int32(0))
+    row, col = positions()
+    x_ref[...] = x_first[...]
+
+    def again(state):
+        error = invert_step(a_ref, x_ref, True)
+        return jnp.sum(error * error), state[1] + 1
+
+    size, _ = lax.while_loop(
+        lambda s: (s[0] > 3e-5) & (s[1] < 40), again, (jnp.float32(1e9), jnp.int32(0))
     )
-    del rough
-    size, _ = lax.while_loop(
-        lambda s: (s[0] > 1e-6) & (s[1] < 40), step(True), (jnp.float32(1e9), jnp.int32(0))
-    )
-
-    @pl.when(jnp.logical_not(size <= 1e-6))
+
+    @pl.when(jnp.logical_not(size <= 3e-5))
     def _():
         w_ref[...] = a_ref[...]
         x_ref[...] = jnp.where(row == col, 1.0, 0.0)
@@ -499,12 +548,12 @@
 
         lax.fori_loop(0, RANK, eliminate, 0)
 
-    inverse = jnp.where(row >= col, x_ref[...], 0.0) * by_col
+    inverse = jnp.where(row >= col, x_ref[...], 0.0) * scale[...]
     x_ref[...] = inverse
     halves = split(inverse)
     squares = jnp.zeros((1, RANK), f32)
     for q in range(4):
-        block = mall[q, :, :FACTOR_ROWS].reshape(BLOCK, RANK)
+        block = mall[q].reshape(BLOCK, RANK)
         factor = dot_split(split(block), halves) * (1.0 / REPLICAS)
         top, rest = split(factor)
         top_ref[q * BLOCK : (q + 1) * BLOCK] = top
@@ -539,7 +588,7 @@
         copy.wait()
 
 
-def finish(buffer, projected, mall):
+def finish(*gathered):
     vmem = pl.BlockSpec(memory_space=VMEM)
     anywhere = pl.BlockSpec(memory_space=pltpu.HBM)
     return pl.pallas_call(
@@ -550,10 +599,9 @@
             jax.ShapeDtypeStruct((SHARD, COLS), jnp.bfloat16),
             jax.ShapeDtypeStruct((OWN, RANK), f32),
         ),
-        in_specs=[vmem] * 3,
+        in_specs=[vmem] * 6,
         out_specs=(anywhere, anywhere, vmem),
         scratch_shapes=[
-            VMEM((RANK, RANK), f32),
             VMEM((RANK, RANK), f32),
             VMEM((RANK, RANK), f32),
             VMEM((COLS, RANK), jnp.bfloat16),
@@ -564,7 +612,7 @@
             pltpu.SemaphoreType.DMA((9,)),
         ],
         compiler_params=pltpu.CompilerParams(vmem_limit_bytes=40 * 1024 * 1024),
-    )(buffer, projected, mall)
+    )(*gathered)
 
 
 def shards(momentum, gradient, right_factor):

time: 95.2 us -> 88.2 us (0.926)
  Pallas kernels: 94.2 us -> 87.4 us
    pallas_call x1, Pallas kernels: 10.6 us -> 5.79 us  [finish(): pl.pallas_call(finish_kernel, name='finish', out_shape=(jax.ShapeDtypeStr...]
    pallas_call x1, Pallas kernels: 83.7 us -> 81.6 us  [exchange(): pl.pallas_call(exchange_kernel, name='exchange', out_shape=(jax.ShapeDtyp...]
where the time goes in v3:
time: 88.2 us; the launch traced here: 88 us
  Pallas kernels  87.4 us (99%)
    pallas_call x1, Pallas kernels, exchange(): pl.pallas_call(exchange_kernel, name='exchange', out_shape=(jax.ShapeDtyp...  81.6 us
    pallas_call x1, Pallas kernels, finish(): pl.pallas_call(finish_kernel, name='finish', out_shape=(jax.ShapeDtypeStr...  5.79 us

profile of v3, /device:TPU:1, one launch (start us, length us, event | category | flops | bytes accessed | tf_op | source)
XLA Modules:
  0.0 88.0 jit_solution(17084484340032746156)
XLA Ops:
  0.6 81.6 %exchange.1 = (f32[144,2304]{1,0:T(8,128)S(1)}, f32[144,256]{1,0:T(8,128)S(1)}, f32[4,8,72,256]{3,2,1,0:T(8,128)S(1)}, f32[256,256]{1,0:T(8,128)S(1)}, f32[256,256]{1,0:T(8,128)S(1)}, /*index=5*/f32[1,256]{1,0:T(1,128)S(1)}) custom-call(f32[1,144,2304]{2,1,0:T(8,128)} %m_hbm.1, bf16[1,144,2304]{2,1,0:T(8,128)(2,1)} %g_hbm.1, f32[18,256]{1,0:T(8,128)} %r_hbm.1), custom_call_target="tpu_custom_call" | custom-call | tf_op jit(solution)/shard_map/exchange/pallas_call | solution.py:456
  82.2 5.8 %finish.1 = (f32[1,144,2304]{2,1,0:T(8,128)}, bf16[144,2304]{1,0:T(8,128)(2,1)}, f32[18,256]{1,0:T(8,128)}) custom-call(f32[144,2304]{1,0:T(8,128)S(1)} %get-tuple-element.9.buffer, f32[144,256]{1,0:T(8,128)S(1)} %get-tuple-element.10.p_ref, f32[4,8,72,256]{3,2,1,0:T(8,128)S(1)} %get-tuple-element.11.mall, f32[256,256]{1,0:T(8,128)S(1)} %get-tuple-element.12.a_ref, ...), custom_call_target="tpu_custom_call" | custom-call | tf_op jit(solution)/shard_map/finish/pallas_call | solution.py:594

commit v4 on v3

--- a/solution.py
+++ b/solution.py
@@ -17,6 +17,7 @@
 NX, NZ = 4, 16
 SHARD = ROWS // 128
 BLOCK = COLS // 4
+PACKED = SHARD * BLOCK // 128
 OWN = COLS // 128
 PIECE = 80
 FACTOR_ROWS = 72
@@ -41,27 +42,26 @@
     )
 
 
-def gather_ring(block, me, right, left, send, recv):
-    before, after, across = (me + 3) % 4, (me + 1) % 4, (me + 2) % 4
+def took(ref, sem, device):
+    copy_to(ref, ref, sem, sem, device).wait_recv()
+
+
+def gather_ring(block, two, three, me, right, left, send, recv, meanwhile):
+    before, after = (me + 3) % 4, (me + 1) % 4
 
     def hop(q, h, device, i):
-        return copy_to(block(q, h), block(q, h), send.at[i], recv.at[i], device)
-
-    first = [hop(me, 0, right, 0), hop(me, 1, left, 1), hop(me, 1, right, 2), hop(me, 0, left, 3)]
+        return copy_to(block(q, h), block(q, h), send.at[0], recv.at[i], device)
+
+    first = [hop(me, 0, right, 0), hop(me, 1, left, 1), hop(me, 1, right, 2), hop(me, 0, left, 2)]
     for copy in first:
         copy.start()
+    meanwhile()
     first[0].wait_recv()
-    onward = hop(before, 0, right, 4)
-    onward.start()
+    hop(before, 0, right, 2).start()
     first[1].wait_recv()
-    backward = hop(after, 1, left, 5)
-    backward.start()
-    first[2].wait_recv()
-    first[3].wait_recv()
-    onward.wait_recv()
-    backward.wait_recv()
-    for copy in first + [onward, backward]:
-        copy.wait_send()
+    hop(after, 1, left, 2).start()
+    took(two, recv.at[2], right)
+    took(three, send.at[0], right)
 
 
 def dot(a, b, contract, precise=True):
@@ -100,8 +100,8 @@
 
 
 def exchange_kernel(
-    m_hbm, g_hbm, r_hbm, buffer, p_out, mall, a_out, x_out, scale,
-    mv, gv, bs, raw, comb, cin, inn, s_c, s_t, rall, rc, pall, gram, mloc, crecv, mx, xrecv, mz, zrecv, fin, zall, gall,
+    m_hbm, g_hbm, r_hbm, buffer, p_out, mall, a_out, x_out, scale, size,
+    mv, gv, bs, raw, comb, cin, inn, packed, s_c, s_t, rall, rc, pall, p_t, mloc, crecv, mx, xrecv, mz, zrecv, fin, zall, gall,
     load, s_send, s_recv, rx_send, rx_recv, rz_send, rz_recv, rc_send, rc_recv, p_send, p_recv,
     c_send, c_recv, x_send, x_recv, z_send, z_recv, f_send, f_recv, a_send, a_recv, b_send, b_recv,
     d_send, d_recv, gx_send, gx_recv, gy_send, gy_recv, gc_send, gc_recv,
@@ -143,7 +143,10 @@
         columns = slice(q * BLOCK, (q + 1) * BLOCK)
         part = mv[:, columns] + gv[:, columns].astype(f32)
         buffer[:, columns] = part
-        bs[q] = part
+        for t in range(4):
+            bs[q, t * SHARD : (t + 1) * SHARD] = part[:, t * 128 : (t + 1) * 128]
+        bs[q, 4 * SHARD :, :64] = part[: SHARD // 2, 512:]
+        bs[q, 4 * SHARD :, 64:] = part[SHARD // 2 :, 512:]
 
     @pl.when(source)
     def _():
@@ -152,7 +155,7 @@
     pl.semaphore_wait(barrier, len(peers))
 
     to_x = [
-        copy_to(rall.at[z, c], rall.at[z, c], rx_send.at[d - 1], rx_recv.at[0], at_x((x + d) % 4))
+        copy_to(rall.at[z, c], rall.at[z, c], rx_send.at[0], rx_recv.at[0], at_x((x + d) % 4))
         for d in range(1, 4)
     ]
 
@@ -162,14 +165,16 @@
             copy.start()
 
     half = SHARD // 2
+    cut = PACKED // 2 // 8 * 8
     up, down = at_y((y + 1) % 4), at_y((y + 3) % 4)
     after, before, across = (y + 1) % 4, (y + 3) % 4, (y + 2) % 4
-    low, high = pl.ds(0, half), pl.ds(half, half)
+    low, high = pl.ds(0, cut), pl.ds(cut, PACKED - cut)
+    rest = pl.ds(0, PACKED - cut)
     sums = [
-        copy_to(bs.at[across, low], raw.at[0], s_send.at[0], s_recv.at[0], up),
-        copy_to(bs.at[across, high], raw.at[1], s_send.at[1], s_recv.at[1], down),
-        copy_to(bs.at[after, high], inn.at[1], s_send.at[2], s_recv.at[2], up),
-        copy_to(bs.at[before, low], inn.at[0], s_send.at[3], s_recv.at[3], down),
+        copy_to(bs.at[across, low], raw.at[0, low], s_send.at[0], s_recv.at[0], up),
+        copy_to(bs.at[across, high], raw.at[1, rest], s_send.at[0], s_recv.at[1], down),
+        copy_to(bs.at[after, high], inn.at[1, rest], s_send.at[0], s_recv.at[2], up),
+        copy_to(bs.at[before, low], inn.at[0, low], s_send.at[0], s_recv.at[2], down),
     ]
     for copy in sums:
         copy.start()
@@ -180,19 +185,20 @@
 
     def along_z(owner, far, step):
         block = rall.at[(z + NZ - owner) % NZ, c]
-        return copy_to(block, block, rz_send.at[far % NZ - 1], rz_recv.at[far % NZ - 1], at_z((z + NZ + step) % NZ))
+        arrival = {4: 0, -4: 1}.get(far, 2)
+        return copy_to(block, block, rz_send.at[0], rz_recv.at[arrival], at_z((z + NZ + step) % NZ))
 
     to_z = [along_z(0, d, d) for d in (4, -4, 3, -3, 2, -2, 1, -1)]
     for copy in to_z:
         copy.start()
 
     sums[0].wait_recv()
-    comb[0] = raw[0] + bs[after, :half]
-    sums.append(copy_to(comb.at[0], cin.at[0], s_send.at[4], s_recv.at[4], up))
+    comb[0, :cut] = raw[0, :cut] + bs[after, :cut]
+    sums.append(copy_to(comb.at[0, low], cin.at[0, low], s_send.at[0], s_recv.at[2], up))
     sums[4].start()
     sums[1].wait_recv()
-    comb[1] = raw[1] + bs[before, half:]
-    sums.append(copy_to(comb.at[1], cin.at[1], s_send.at[5], s_recv.at[5], down))
+    comb[1, : PACKED - cut] = raw[1, : PACKED - cut] + bs[before, cut:]
+    sums.append(copy_to(comb.at[1, rest], cin.at[1, rest], s_send.at[0], s_recv.at[2], down))
     sums[5].start()
 
     to_z[0].wait_recv()
@@ -204,16 +210,16 @@
     for copy in beyond[4:]:
         copy.start()
 
-    for copy in sums[2:]:
-        copy.wait_recv()
-    s_c[:half] = bs[y, :half] + inn[0] + cin[0]
-    s_c[half:] = bs[y, half:] + inn[1] + cin[1]
-    s_t[...] = s_c[...].T
-
-    for copy in to_z[2:] + beyond:
-        copy.wait_recv()
+    took(rall.at[pl.ds(0, 13), c], rz_recv.at[2], partner)
     over = copy_to(rall.at[:, c], rall.at[:, c], rc_send.at[0], rc_recv.at[0], partner)
     over.start()
+    took(bs.at[pl.ds(0, 2)], s_recv.at[2], up)
+    packed[:cut] = bs[y, :cut] + inn[0, :cut] + cin[0, :cut]
+    packed[cut:] = bs[y, cut:] + inn[1, : PACKED - cut] + cin[1, : PACKED - cut]
+    for t in range(4):
+        s_c[:, t * 128 : (t + 1) * 128] = packed[t * SHARD : (t + 1) * SHARD]
+    s_c[: SHARD // 2, 512:] = packed[4 * SHARD :, :64]
+    s_c[SHARD // 2 :, 512:] = packed[4 * SHARD :, 64:]
     over.wait_recv()
     for b in range(32):
         rc[b * OWN : (b + 1) * OWN] = rall[b // 2, b % 2]
@@ -222,71 +228,83 @@
     def rows_of(q, h):
         return pall.at[q, pl.ds(half * h, half)]
 
-    gather_ring(rows_of, y, up, down, p_send, p_recv)
+    def turn():
+        s_t[...] = s_c[...].T
+
+    gather_ring(
+        rows_of, pall.at[pl.ds(0, 2)], pall.at[pl.ds(0, 3)], y, up, down, p_send, p_recv, turn
+    )
     projected = pall[0] + pall[1] + pall[2] + pall[3]
     p_out[...] = projected
 
-    along_rows = (((0,), (0,)), ((), ()))
-    gram[...] = lax.dot_general(projected, projected, along_rows, precision=highest, preferred_element_type=f32)
+    p_t[...] = projected.T
 
     def fill(side):
-        rows = pl.ds(pl.multiple_of(4 * FACTOR_ROWS * side, 8), 4 * FACTOR_ROWS)
-        part = jnp.dot(s_t[rows, :], projected, precision=highest, preferred_element_type=f32)
+        wide, narrow = 4 * FACTOR_ROWS, 32
+        rows = pl.ds(pl.multiple_of(wide * side, 8), wide)
+        gram_rows = pl.ds(pl.multiple_of(2 * narrow * y + narrow * side, 8), narrow)
+        left = jnp.concatenate([s_t[rows, :], p_t[gram_rows, :]], axis=0)
+        part = jnp.dot(left, projected, precision=highest, preferred_element_type=f32)
         for i in range(4):
             mloc[4 * side + i, :FACTOR_ROWS] = part[i * FACTOR_ROWS : (i + 1) * FACTOR_ROWS]
-            mloc[4 * side + i, FACTOR_ROWS:] = gram[
-                pl.ds(pl.multiple_of(64 * y + 8 * (4 * side + i), 8), 8), :
-            ]
+            mloc[4 * side + i, FACTOR_ROWS:] = part[wide + 8 * i : wide + 8 * i + 8]
 
     fill(1 - c)
     to_core = copy_to(mloc.at[pl.ds(4 * (1 - c), 4)], crecv, c_send.at[0], c_recv.at[0], partner)
     to_core.start()
     fill(c)
     to_core.wait_recv()
-    sums_x = [
-        copy_to(mx.at[(x + d) % 4], xrecv.at[d - 1], x_send.at[d - 1], x_recv.at[d - 1], at_x((x + d) % 4))
-        for d in (2, 1, 3)
-    ]
-    for d, copy in zip((2, 1, 3), sums_x, strict=True):
+    factor_rows, gram_rows = pl.ds(0, FACTOR_ROWS), pl.ds(FACTOR_ROWS, 8)
+
+    def along_x(d, part, i):
         q = (x + d) % 4
+        return copy_to(mx.at[q, part], xrecv.at[d - 1, part], x_send.at[0], x_recv.at[i], at_x(q))
+
+    sums_g = [along_x(d, gram_rows, 0) for d in (2, 1, 3)]
+    sums_x = [along_x(d, factor_rows, 1) for d in (2, 1, 3)]
+    for q in range(4):
         mx[q] = mloc[4 * c + q] + crecv[q]
-        copy.start()
-    mx[x] = mloc[4 * c + x] + crecv[x]
-    for copy in sums_x:
-        copy.wait_recv()
-    mz[...] = mx[x] + xrecv[0] + xrecv[1] + xrecv[2]
+    for copy in sums_g + sums_x:
+        copy.start()
 
     owners = [(16 * t + 9) // 10 for t in range(TILES)]
     tile = (z * TILES) // NZ
     owner = (z * TILES) % NZ < TILES
     sums_z = [
-        copy_to(mz.at[pl.ds(8 * t, 8)], zrecv.at[z], z_send.at[t], z_recv.at[z], at_z(owners[t]))
+        copy_to(mz.at[pl.ds(8 * t, 8)], zrecv.at[z], z_send.at[0], z_recv.at[0], at_z(owners[t]))
         for t in range(TILES)
     ]
-    for t in range(TILES):
-
+
+    def to_owner(t):
         @pl.when(z != owners[t])
         def _():
             sums_z[t].start()
+
+    took(mz.at[pl.ds(0, 24)], x_recv.at[0], partner)
+    mz[FACTOR_ROWS:] = (
+        mx[x, FACTOR_ROWS:] + xrecv[0, FACTOR_ROWS:] + xrecv[1, FACTOR_ROWS:] + xrecv[2, FACTOR_ROWS:]
+    )
+    to_owner(TILES - 1)
+    took(mall.at[0, pl.ds(0, 3)], x_recv.at[1], partner)
+    mz[:FACTOR_ROWS] = (
+        mx[x, :FACTOR_ROWS] + xrecv[0, :FACTOR_ROWS] + xrecv[1, :FACTOR_ROWS] + xrecv[2, :FACTOR_ROWS]
+    )
+    for t in range(TILES - 1):
+        to_owner(t)
 
     group = 4 * c + x
     rows = pl.ds(pl.multiple_of(8 * tile, 8), 8)
     to_all = [
         copy_to(
-            fin, zall.at[rows], f_send.at[d - 1], f_recv.at[tile], at_z((z + d) % NZ)
+            fin, zall.at[rows], f_send.at[0], f_recv.at[tile // (TILES - 1)], at_z((z + d) % NZ)
         )
         for d in sorted(range(1, NZ), key=lambda d: abs(d - NZ // 2))
     ]
 
     @pl.when(owner)
     def _():
+        took(zrecv.at[pl.ds(0, NZ - 1)], z_recv.at[0], partner)
         zrecv[z] = mz[rows, :]
-        for s in range(NZ):
-
-            @pl.when(z != s)
-            def _():
-                copy_to(zrecv.at[s], zrecv.at[s], z_send.at[0], z_recv.at[s], partner).wait_recv()
-
         total = zrecv[0]
         for s in range(1, NZ):
             total = total + zrecv[s]
@@ -295,30 +313,40 @@
             copy.start()
         zall[rows, :] = total
 
-    def tile_here(t):
-        @pl.when(z != owners[t])
-        def _():
-            copy_to(fin, zall.at[pl.ds(8 * t, 8)], f_send.at[0], f_recv.at[t], partner).wait_recv()
-
-    tile_here(TILES - 1)
-    gram_rows = pl.ds(FACTOR_ROWS, 8)
+    last = owners[-1]
+
+    @pl.when(z != last)
+    def _():
+        took(fin, f_recv.at[1], partner)
+
     gram_x = [
         copy_to(
-            zall.at[gram_rows], gall.at[y, group], gx_send.at[d - 1], gx_recv.at[d - 1], at_x((x + d) % 4)
+            zall.at[gram_rows], gall.at[y, group], gx_send.at[0], gx_recv.at[0], at_x((x + d) % 4)
         )
         for d in (2, 1, 3)
     ]
     mine = pl.ds(4 * c, 4)
     gram_y = [
-        copy_to(gall.at[y, mine], gall.at[y, mine], gy_send.at[d - 1], gy_recv.at[d - 1], at_y((y + d) % 4))
+        copy_to(gall.at[y, mine], gall.at[y, mine], gy_send.at[0], gy_recv.at[0], at_y((y + d) % 4))
         for d in (2, 1, 3)
     ]
     gram_core = copy_to(gall.at[:, mine], gall.at[:, mine], gc_send.at[0], gc_recv.at[0], partner)
     for copy in gram_x:
         copy.start()
     gall[y, group] = zall[gram_rows, :]
-    for t in range(TILES - 1):
-        tile_here(t)
+    took(gall.at[y, pl.ds(0, 3)], gx_recv.at[0], partner)
+    for copy in gram_y:
+        copy.start()
+    owns_factor = owner & (z != last)
+
+    @pl.when(owns_factor)
+    def _():
+        took(zall.at[pl.ds(0, FACTOR_ROWS - 8)], f_recv.at[0], partner)
+
+    @pl.when(jnp.logical_not(owns_factor))
+    def _():
+        took(zall.at[pl.ds(0, FACTOR_ROWS)], f_recv.at[0], partner)
+
 
     first, second = x * (1 - c) + y * c, y * (1 - c) + x * c
 
@@ -338,20 +366,18 @@
 
     def on_first(k, h, step, i):
         device = turned((first + step) % 4, second) + (z, c)
-        return copy_to(source_of(k, 0, h), half_of(k, 0, h), a_send.at[i], a_recv.at[i], device)
+        return copy_to(source_of(k, 0, h), half_of(k, 0, h), a_send.at[0], a_recv.at[i], device)
 
     def on_second(k, j, h, step, i):
         device = turned(first, (second + step) % 4) + (z, c)
-        i = 6 * k + i
-        return copy_to(source_of(k, j, h), half_of(k, j, h), b_send.at[i], b_recv.at[i], device)
+        return copy_to(source_of(k, j, h), half_of(k, j, h), b_send.at[0], b_recv.at[3 * k + min(i, 2)], device)
 
     def on_chip(k, j):
-        i = 4 * k + j
         source = block_of(k, j) if k or j else zall.at[pl.ds(0, FACTOR_ROWS)]
-        return copy_to(source, block_of(k, j), d_send.at[i], d_recv.at[i], partner)
+        return copy_to(source, block_of(k, j), d_send.at[0], d_recv.at[0], partner)
 
     ring = [on_first(0, 0, 1, 0), on_first(0, 1, 3, 1), on_first(0, 1, 1, 2), on_first(0, 0, 3, 3)]
-    ring += [on_first(3, 0, 1, 4), on_first(1, 1, 3, 5)]
+    ring += [on_first(0, 0, 2, 4), on_first(0, 1, 2, 5)]
     across_ring = [
         [on_second(k, 0, 0, 1, 0), on_second(k, 0, 1, 3, 1), on_second(k, 0, 1, 1, 2)]
         + [on_second(k, 0, 0, 3, 3), on_second(k, 3, 0, 1, 4), on_second(k, 1, 1, 3, 5)]
@@ -369,26 +395,21 @@
             across_ring[k][4 + i].start()
 
     def complete(k):
-        for i in range(2, 6):
-            across_ring[k][i].wait_recv()
+        took(mall.at[pl.ds(0, 2), 0], b_recv.at[3 * k + 2], partner)
         for j in range(1, 4):
             cores[k][j].start()
 
-    for copy in ring[:4]:
+    for copy in ring[4:] + ring[:4]:
         copy.start()
     start_half(0, 0)
     start_half(0, 1)
     cores[0][0].start()
     mall[y, group] = zall[:FACTOR_ROWS, :]
-    for copy in gram_x:
-        copy.wait_recv()
-    for copy in gram_y:
-        copy.start()
+    took(gall.at[pl.ds(0, 3), pl.ds(0, 4)], gy_recv.at[0], partner)
+    gram_core.start()
     ring[0].wait_recv()
-    ring[4].start()
     start_half(3, 0)
     ring[1].wait_recv()
-    ring[5].start()
     start_half(1, 1)
     ring[2].wait_recv()
     start_half(3, 1)
@@ -396,63 +417,64 @@
     start_half(1, 0)
     cores[3][0].start()
     cores[1][0].start()
-    for copy in gram_y:
-        copy.wait_recv()
-    gram_core.start()
-    hand_on(0)
+    gram_core.wait_recv()
+    invert_start(gall[...].reshape(RANK, RANK), a_out, x_out, scale)
+    invert_step(a_out, x_out, False)
     ring[4].wait_recv()
     start_half(2, 0)
     ring[5].wait_recv()
     start_half(2, 1)
     cores[2][0].start()
+    hand_on(0)
+    for _ in range(2):
+        invert_step(a_out, x_out, False)
     hand_on(3)
     hand_on(1)
-    gram_core.wait_recv()
-    invert_start(gall[...].reshape(RANK, RANK), a_out, x_out, scale)
-    invert_step(a_out, x_out, False)
-    invert_step(a_out, x_out, False)
+    for _ in range(2):
+        invert_step(a_out, x_out, False)
+    hand_on(2)
     complete(0)
-    invert_step(a_out, x_out, False)
-    hand_on(2)
-    invert_step(a_out, x_out, False)
-    invert_step(a_out, x_out, False)
+    for _ in range(2):
+        invert_step(a_out, x_out, False)
     complete(3)
-    invert_step(a_out, x_out, False)
     complete(1)
-    invert_step(a_out, x_out, False)
     invert_step(a_out, x_out, True)
     complete(2)
+    error = invert_step(a_out, x_out, True)
+    size[...] = jnp.sum(jnp.sum(error * error, axis=0, keepdims=True), axis=1, keepdims=True)
 
     @pl.when(source)
     def _():
-        for copy in to_x:
-            copy.wait_send()
-
-    for copy in to_z + beyond + sums + [over, to_core, gram_core] + sums_x + ring + gram_x + gram_y:
-        copy.wait_send()
-    for t in range(TILES):
-
-        @pl.when(z != owners[t])
-        def _():
-            sums_z[t].wait_send()
+        took(rall.at[pl.ds(0, 3), c], rx_send.at[0], partner)
+
+    took(rall.at[pl.ds(0, 15), c], rz_send.at[0], partner)
+    took(bs.at[pl.ds(0, 3)], s_send.at[0], partner)
+    over.wait_send()
+    to_core.wait_send()
+    took(mx.at[pl.ds(0, 3)], x_send.at[0], partner)
 
     @pl.when(owner)
     def _():
-        for copy in to_all:
-            copy.wait_send()
-
-    for k in range(4):
-        for copy in across_ring[k] + cores[k]:
-            copy.wait_send()
-    for k in range(4):
-        for copy in cores[k]:
-            copy.wait_recv()
+        took(zall.at[pl.ds(0, PIECE - 8)], z_send.at[0], partner)
+        took(zrecv.at[pl.ds(0, NZ - 1)], f_send.at[0], partner)
+
+    @pl.when(jnp.logical_not(owner))
+    def _():
+        took(zall, z_send.at[0], partner)
+
+    took(gall.at[y, pl.ds(0, 3)], gx_send.at[0], partner)
+    took(gall.at[pl.ds(0, 3), pl.ds(0, 4)], gy_send.at[0], partner)
+    gram_core.wait_send()
+    took(mall.at[pl.ds(0, 3), 0], a_send.at[0], partner)
+    took(mall.at[pl.ds(0, 3), pl.ds(0, 4)], b_send.at[0], partner)
+    took(mall.at[:, pl.ds(0, 4)], d_send.at[0], partner)
+    took(mall.at[:, pl.ds(0, 4)], d_recv.at[0], partner)
 
 
 def exchange(momentum, gradient, right_factor):
     sem = pltpu.SemaphoreType.DMA
-    half = SHARD // 2
-    counts = (3, 6, 6, 3, 1, 15, 15, 1, 1, 6, 6, 1, 1, 3, 3, TILES, NZ, 15, TILES, 6, 6, 24, 24, 16, 16, 3, 3, 3, 3, 1, 1)
+    longer = PACKED - PACKED // 2 // 8 * 8
+    counts = (3, 1, 3, 1, 1, 1, 3, 1, 1, 1, 3, 1, 1, 1, 2, 1, 1, 1, 2, 1, 6, 1, 12) + (1,) * 8
     return pl.pallas_call(
         exchange_kernel,
         name="exchange",
@@ -463,23 +485,25 @@
             jax.ShapeDtypeStruct((RANK, RANK), f32),
             jax.ShapeDtypeStruct((RANK, RANK), f32),
             jax.ShapeDtypeStruct((1, RANK), f32),
+            jax.ShapeDtypeStruct((1, 1), f32),
         ),
         in_specs=[pl.BlockSpec(memory_space=pltpu.HBM)] * 3,
-        out_specs=(pl.BlockSpec(memory_space=VMEM),) * 6,
+        out_specs=(pl.BlockSpec(memory_space=VMEM),) * 7,
         scratch_shapes=[
             VMEM((SHARD, COLS), f32),
             VMEM((SHARD, COLS), jnp.bfloat16),
-            VMEM((4, SHARD, BLOCK), f32),
-            VMEM((2, half, BLOCK), f32),
-            VMEM((2, half, BLOCK), f32),
-            VMEM((2, half, BLOCK), f32),
-            VMEM((2, half, BLOCK), f32),
+            VMEM((4, PACKED, 128), f32),
+            VMEM((2, longer, 128), f32),
+            VMEM((2, longer, 128), f32),
+            VMEM((2, longer, 128), f32),
+            VMEM((2, longer, 128), f32),
+            VMEM((PACKED, 128), f32),
             VMEM((SHARD, BLOCK), f32),
             VMEM((BLOCK, SHARD), f32),
             VMEM((NZ, 2, OWN, RANK), f32),
             VMEM((BLOCK, RANK), f32),
             VMEM((4, SHARD, RANK), f32),
-            VMEM((RANK, RANK), f32),
+            VMEM((RANK, SHARD), f32),
             VMEM((8, PIECE, RANK), f32),
             VMEM((4, PIECE, RANK), f32),
             VMEM((4, PIECE, RANK), f32),
@@ -513,7 +537,7 @@
 
 
 def finish_kernel(
-    buffer, p_ref, mall, a_ref, x_first, scale, new_m, update, new_f,
+    buffer, p_ref, mall, a_ref, x_first, scale, first_size, new_m, update, new_f,
     x_ref, w_ref, top_ref, rest_ref, m_buf, u_buf, m_sem, u_sem,
 ):
     x, z, c = (lax.axis_index(name) for name in FSDP)
@@ -526,7 +550,7 @@
         return jnp.sum(error * error), state[1] + 1
 
     size, _ = lax.while_loop(
-        lambda s: (s[0] > 3e-5) & (s[1] < 40), again, (jnp.float32(1e9), jnp.int32(0))
+        lambda s: jnp.logical_not(s[0] <= 3e-5) & (s[1] < 40), again, (jnp.max(first_size[...]), jnp.int32(0))
     )
 
     @pl.when(jnp.logical_not(size <= 3e-5))
@@ -599,7 +623,7 @@
             jax.ShapeDtypeStruct((SHARD, COLS), jnp.bfloat16),
             jax.ShapeDtypeStruct((OWN, RANK), f32),
         ),
-        in_specs=[vmem] * 6,
+        in_specs=[vmem] * 7,
         out_specs=(anywhere, anywhere, vmem),
         scratch_shapes=[
             VMEM((RANK, RANK), f32),

time: 88.2 us -> 85.5 us (0.969)
  Pallas kernels: 87.4 us -> 84.7 us
    pallas_call x1, Pallas kernels: 81.6 us -> 79.6 us  [exchange(): pl.pallas_call(exchange_kernel, name='exchange', out_shape=(jax.ShapeDtyp...]
where the time goes in v4:
time: 85.5 us; the launch traced here: 85.3 us
  Pallas kernels  84.7 us (99%)
    pallas_call x1, Pallas kernels, exchange(): pl.pallas_call(exchange_kernel, name='exchange', out_shape=(jax.ShapeDtyp...  79.6 us
    pallas_call x1, Pallas kernels, finish(): pl.pallas_call(finish_kernel, name='finish', out_shape=(jax.ShapeDtypeStr...  5.05 us

profile of v4, /device:TPU:1, one launch (start us, length us, event | category | flops | bytes accessed | tf_op | source)
XLA Modules:
  0.0 85.3 jit_solution(4119792477481030504)
XLA Ops:
  0.6 79.6 %exchange.1 = (f32[144,2304]{1,0:T(8,128)S(1)}, f32[144,256]{1,0:T(8,128)S(1)}, f32[4,8,72,256]{3,2,1,0:T(8,128)S(1)}, f32[256,256]{1,0:T(8,128)S(1)}, f32[256,2...) custom-call(f32[1,144,2304]{2,1,0:T(8,128)} %m_hbm.1, bf16[1,144,2304]{2,1,0:T(8,128)(2,1)} %g_hbm.1, ...), custom_call_target="tpu_custom_call" | custom-call | tf_op jit(solution)/shard_map/exchange/pallas_call | solution.py:478
  80.3 5.1 %finish.1 = (f32[1,144,2304]{2,1,0:T(8,128)}, bf16[144,2304]{1,0:T(8,128)(2,1)}, f32[18,256]{1,0:T(8,128)}) custom-call(f32[144,2304]{1,0:T(8,128)S(1)} %get-tuple-element.10.buffer, f32[144,256]{1,0:T(8,128)S(1)} %get-tuple-element.11.p_ref, f32[4,8,72,256]{3,2,1,0:T(8,128)S(1)} %get-tuple-element.12.mall, f32[256,256]{1,0:T(8,128)S(1)} %get-tuple-element.13.a_ref, ...), custom_call_target="tpu_custom_call" | custom-call | tf_op jit(solution)/shard_map/finish/pallas_call | solution.py:618

commit v5 on v4

--- a/solution.py
+++ b/solution.py
@@ -64,12 +64,24 @@
     took(three, send.at[0], right)
 
 
-def dot(a, b, contract, precise=True):
-    if not precise:
-        a, b = a.astype(jnp.bfloat16), b.astype(jnp.bfloat16)
-    return lax.dot_general(
-        a, b, (contract, ((), ())), precision=highest if precise else None, preferred_element_type=f32
-    )
+def split(a):
+    top = a.astype(jnp.bfloat16)
+    return top, (a - top.astype(f32)).astype(jnp.bfloat16)
+
+
+ROUGH, FAIR, FULL = 0, 1, 2
+
+
+def dot(a, b, contract, mode=FULL):
+    def product(left, right):
+        return lax.dot_general(left, right, (contract, ((), ())), preferred_element_type=f32)
+
+    if mode == FULL:
+        return lax.dot_general(a, b, (contract, ((), ())), precision=highest, preferred_element_type=f32)
+    if mode == ROUGH:
+        return product(a.astype(jnp.bfloat16), b.astype(jnp.bfloat16))
+    (a_top, a_rest), (b_top, b_rest) = split(a), split(b)
+    return product(a_top, b_top) + (product(a_top, b_rest) + product(a_rest, b_top))
 
 
 def positions():
@@ -86,22 +98,22 @@
     a_ref[...] = scaled
     scale[...] = by_col
     bound = jnp.max(jnp.sum(jnp.abs(scaled), axis=0, keepdims=True), axis=1, keepdims=True)
-    x_ref[...] = jnp.where(row == col, lax.rsqrt(bound / 1.5), 0.0)
-
-
-def invert_step(a_ref, x_ref, precise):
+    x_ref[...] = jnp.where(row == col, lax.rsqrt(bound / 2.0), 0.0)
+
+
+def invert_step(a_ref, x_ref, mode, last=FULL):
     row, col = positions()
     inverse = x_ref[...]
-    error = dot(dot(inverse, a_ref[...], ((1,), (0,)), precise), inverse, ((1,), (1,)), precise)
+    error = dot(dot(inverse, a_ref[...], ((1,), (0,)), mode), inverse, ((1,), (1,)), mode)
     error = jnp.where(row == col, error - 1.0, error)
     lower = jnp.where(row > col, error, jnp.where(row == col, 0.5 * error, 0.0))
-    x_ref[...] = inverse - dot(lower, inverse, ((1,), (0,)), precise)
+    x_ref[...] = inverse - dot(lower, inverse, ((1,), (0,)), last)
     return error
 
 
 def exchange_kernel(
     m_hbm, g_hbm, r_hbm, buffer, p_out, mall, a_out, x_out, scale, size,
-    mv, gv, bs, raw, comb, cin, inn, packed, s_c, s_t, rall, rc, pall, p_t, mloc, crecv, mx, xrecv, mz, zrecv, fin, zall, gall,
+    mv, gv, rv, bs, raw, comb, cin, inn, packed, s_c, s_t, rall, rc, pall, p_t, mloc, crecv, mx, xrecv, mz, zrecv, fin, zall, gall,
     load, s_send, s_recv, rx_send, rx_recv, rz_send, rz_recv, rc_send, rc_recv, p_send, p_recv,
     c_send, c_recv, x_send, x_recv, z_send, z_recv, f_send, f_recv, a_send, a_recv, b_send, b_recv,
     d_send, d_recv, gx_send, gx_recv, gy_send, gy_recv, gc_send, gc_recv,
@@ -125,7 +137,7 @@
     source = x == y
     load_m = pltpu.make_async_copy(m_hbm.at[0], mv, load.at[0])
     load_g = pltpu.make_async_copy(g_hbm.at[0], gv, load.at[1])
-    load_r = pltpu.make_async_copy(r_hbm, rall.at[z, c], load.at[2])
+    load_r = pltpu.make_async_copy(r_hbm, rv, load.at[2])
 
     @pl.when(source)
     def _():
@@ -151,6 +163,8 @@
     @pl.when(source)
     def _():
         load_r.wait()
+        rall[z, c, :OWN] = rv[:, :128]
+        rall[z, c, OWN:] = rv[:, 128:]
 
     pl.semaphore_wait(barrier, len(peers))
 
@@ -201,14 +215,14 @@
     sums.append(copy_to(comb.at[1, rest], cin.at[1, rest], s_send.at[0], s_recv.at[2], down))
     sums[5].start()
 
-    to_z[0].wait_recv()
-    beyond = [along_z(4, 4 + d, d) for d in (4, 3, 2, 1)]
-    for copy in beyond:
-        copy.start()
-    to_z[1].wait_recv()
-    beyond += [along_z(-4, -4 - d, -d) for d in (3, 2, 1)]
-    for copy in beyond[4:]:
-        copy.start()
+    def hand_along(owner, steps):
+        sign = 1 if owner > 0 else -1
+        along_z(0, owner, sign).wait_recv()
+        for d in steps:
+            along_z(owner, owner + sign * d, sign * d).start()
+
+    hand_along(4, (4, 3, 2, 1))
+    hand_along(-4, (3, 2, 1))
 
     took(rall.at[pl.ds(0, 13), c], rz_recv.at[2], partner)
     over = copy_to(rall.at[:, c], rall.at[:, c], rc_send.at[0], rc_recv.at[0], partner)
@@ -222,7 +236,8 @@
     s_c[SHARD // 2 :, 512:] = packed[4 * SHARD :, 64:]
     over.wait_recv()
     for b in range(32):
-        rc[b * OWN : (b + 1) * OWN] = rall[b // 2, b % 2]
+        rc[b * OWN : (b + 1) * OWN, :128] = rall[b // 2, b % 2, :OWN]
+        rc[b * OWN : (b + 1) * OWN, 128:] = rall[b // 2, b % 2, OWN:]
     pall[y] = jnp.dot(s_c[...], rc[...], precision=highest, preferred_element_type=f32)
 
     def rows_of(q, h):
@@ -370,11 +385,14 @@
 
     def on_second(k, j, h, step, i):
         device = turned(first, (second + step) % 4) + (z, c)
-        return copy_to(source_of(k, j, h), half_of(k, j, h), b_send.at[0], b_recv.at[3 * k + min(i, 2)], device)
+        return copy_to(source_of(k, j, h), half_of(k, j, h), b_send.at[0], b_recv.at[4 * k + (0, 1, 2, 2, 3, 3)[i]], device)
 
     def on_chip(k, j):
         source = block_of(k, j) if k or j else zall.at[pl.ds(0, FACTOR_ROWS)]
-        return copy_to(source, block_of(k, j), d_send.at[0], d_recv.at[0], partner)
+        copy_to(source, block_of(k, j), d_send.at[0], d_recv.at[0], partner).start()
+
+    def half_on_chip(k, j, h):
+        copy_to(half_of(k, j, h), half_of(k, j, h), d_send.at[0], d_recv.at[0], partner).start()
 
     ring = [on_first(0, 0, 1, 0), on_first(0, 1, 3, 1), on_first(0, 1, 1, 2), on_first(0, 0, 3, 3)]
     ring += [on_first(0, 0, 2, 4), on_first(0, 1, 2, 5)]
@@ -383,7 +401,6 @@
         + [on_second(k, 0, 0, 3, 3), on_second(k, 3, 0, 1, 4), on_second(k, 1, 1, 3, 5)]
         for k in range(4)
     ]
-    cores = [[on_chip(k, j) for j in range(4)] for k in range(4)]
 
     def start_half(k, h):
         for i in ((0, 3), (1, 2))[h]:
@@ -393,17 +410,22 @@
         for i in range(2):
             across_ring[k][i].wait_recv()
             across_ring[k][4 + i].start()
+            half_on_chip(k, (3, 1)[i], i)
+
+    def beside(k):
+        took(mall.at[0, 0], b_recv.at[4 * k + 2], partner)
+        half_on_chip(k, 3, 1)
+        half_on_chip(k, 1, 0)
 
     def complete(k):
-        took(mall.at[pl.ds(0, 2), 0], b_recv.at[3 * k + 2], partner)
-        for j in range(1, 4):
-            cores[k][j].start()
+        took(mall.at[0, 0], b_recv.at[4 * k + 3], partner)
+        on_chip(k, 2)
 
     for copy in ring[4:] + ring[:4]:
         copy.start()
     start_half(0, 0)
     start_half(0, 1)
-    cores[0][0].start()
+    on_chip(0, 0)
     mall[y, group] = zall[:FACTOR_ROWS, :]
     took(gall.at[pl.ds(0, 3), pl.ds(0, 4)], gy_recv.at[0], partner)
     gram_core.start()
@@ -415,32 +437,34 @@
     start_half(3, 1)
     ring[3].wait_recv()
     start_half(1, 0)
-    cores[3][0].start()
-    cores[1][0].start()
+    on_chip(3, 0)
+    on_chip(1, 0)
     gram_core.wait_recv()
     invert_start(gall[...].reshape(RANK, RANK), a_out, x_out, scale)
-    invert_step(a_out, x_out, False)
+    invert_step(a_out, x_out, ROUGH, ROUGH)
     ring[4].wait_recv()
     start_half(2, 0)
     ring[5].wait_recv()
     start_half(2, 1)
-    cores[2][0].start()
+    on_chip(2, 0)
     hand_on(0)
-    for _ in range(2):
-        invert_step(a_out, x_out, False)
+    for _ in range(3):
+        invert_step(a_out, x_out, ROUGH, ROUGH)
+    beside(0)
     hand_on(3)
     hand_on(1)
     for _ in range(2):
-        invert_step(a_out, x_out, False)
+        invert_step(a_out, x_out, ROUGH, ROUGH)
+    beside(3)
+    beside(1)
     hand_on(2)
     complete(0)
-    for _ in range(2):
-        invert_step(a_out, x_out, False)
+    invert_step(a_out, x_out, FAIR, ROUGH)
+    beside(2)
     complete(3)
     complete(1)
-    invert_step(a_out, x_out, True)
     complete(2)
-    error = invert_step(a_out, x_out, True)
+    error = invert_step(a_out, x_out, FULL, FAIR)
     size[...] = jnp.sum(jnp.sum(error * error, axis=0, keepdims=True), axis=1, keepdims=True)
 
     @pl.when(source)
@@ -474,7 +498,7 @@
 def exchange(momentum, gradient, right_factor):
     sem = pltpu.SemaphoreType.DMA
     longer = PACKED - PACKED // 2 // 8 * 8
-    counts = (3, 1, 3, 1, 1, 1, 3, 1, 1, 1, 3, 1, 1, 1, 2, 1, 1, 1, 2, 1, 6, 1, 12) + (1,) * 8
+    counts = (3, 1, 3, 1, 1, 1, 3, 1, 1, 1, 3, 1, 1, 1, 2, 1, 1, 1, 2, 1, 6, 1, 16) + (1,) * 8
     return pl.pallas_call(
         exchange_kernel,
         name="exchange",
@@ -492,6 +516,7 @@
         scratch_shapes=[
             VMEM((SHARD, COLS), f32),
             VMEM((SHARD, COLS), jnp.bfloat16),
+            VMEM((OWN, RANK), f32),
             VMEM((4, PACKED, 128), f32),
             VMEM((2, longer, 128), f32),
             VMEM((2, longer, 128), f32),
@@ -500,7 +525,7 @@
             VMEM((PACKED, 128), f32),
             VMEM((SHARD, BLOCK), f32),
             VMEM((BLOCK, SHARD), f32),
-            VMEM((NZ, 2, OWN, RANK), f32),
+            VMEM((NZ, 2, 2 * OWN, 128), f32),
             VMEM((BLOCK, RANK), f32),
             VMEM((4, SHARD, RANK), f32),
             VMEM((RANK, SHARD), f32),
@@ -521,11 +546,6 @@
     )(*(pltpu.with_memory_space_constraint(a, pltpu.HBM) for a in (momentum, gradient, right_factor)))
 
 
-def split(a):
-    top = a.astype(jnp.bfloat16)
-    return top, (a - top.astype(f32)).astype(jnp.bfloat16)
-
-
 def dot_split(a, b):
     (a_top, a_rest), (b_top, b_rest) = a, b
     turn = (((1,), (1,)), ((), ()))
@@ -546,7 +566,7 @@
     x_ref[...] = x_first[...]
 
     def again(state):
-        error = invert_step(a_ref, x_ref, True)
+        error = invert_step(a_ref, x_ref, FULL)
         return jnp.sum(error * error), state[1] + 1
 
     size, _ = lax.while_loop(
@@ -574,11 +594,11 @@
 
     inverse = jnp.where(row >= col, x_ref[...], 0.0) * scale[...]
     x_ref[...] = inverse
-    halves = split(inverse)
+    halves = split(inverse * (1.0 / REPLICAS))
     squares = jnp.zeros((1, RANK), f32)
     for q in range(4):
         block = mall[q].reshape(BLOCK, RANK)
-        factor = dot_split(split(block), halves) * (1.0 / REPLICAS)
+        factor = dot_split(split(block), halves)
         top, rest = split(factor)
         top_ref[q * BLOCK : (q + 1) * BLOCK] = top
         rest_ref[q * BLOCK : (q + 1) * BLOCK] = rest

time: 85.5 us -> 83.1 us (0.972)
  Pallas kernels: 84.7 us -> 81.4 us
    pallas_call x1, Pallas kernels: 79.6 us -> 76.4 us  [exchange(): pl.pallas_call(exchange_kernel, name='exchange', out_shape=(jax.ShapeDtyp...]
where the time goes in v5:
time: 83.1 us; the launch traced here: 82.1 us
  Pallas kernels  81.4 us (98%)
    pallas_call x1, Pallas kernels, exchange(): pl.pallas_call(exchange_kernel, name='exchange', out_shape=(jax.ShapeDtyp...  76.4 us
    pallas_call x1, Pallas kernels, finish(): pl.pallas_call(finish_kernel, name='finish', out_shape=(jax.ShapeDtypeStr...  5.01 us

profile of v5, /device:TPU:1, one launch (start us, length us, event | category | flops | bytes accessed | tf_op | source)
XLA Modules:
  0.0 82.1 jit_solution(169814489011830188)
XLA Ops:
  0.6 76.4 %exchange.1 = (f32[144,2304]{1,0:T(8,128)S(1)}, f32[144,256]{1,0:T(8,128)S(1)}, f32[4,8,72,256]{3,2,1,0:T(8,128)S(1)}, f32[256,256]{1,0:T(8,128)S(1)}, f32[256,2...) custom-call(f32[1,144,2304]{2,1,0:T(8,128)} %m_hbm.1, bf16[1,144,2304]{2,1,0:T(8,128)(2,1)} %g_hbm.1, ...), custom_call_target="tpu_custom_call" | custom-call | tf_op jit(solution)/shard_map/exchange/pallas_call | solution.py:502
  77.0 5.0 %finish.1 = (f32[1,144,2304]{2,1,0:T(8,128)}, bf16[144,2304]{1,0:T(8,128)(2,1)}, f32[18,256]{1,0:T(8,128)}) custom-call(f32[144,2304]{1,0:T(8,128)S(1)} %get-tuple-element.10.buffer, f32[144,256]{1,0:T(8,128)S(1)} %get-tuple-element.11.p_ref, f32[4,8,72,256]{3,2,1,0:T(8,128)S(1)} %get-tuple-element.12.mall, f32[256,256]{1,0:T(8,128)S(1)} %get-tuple-element.13.a_ref, ...), custom_call_target="tpu_custom_call" | custom-call | tf_op jit(solution)/shard_map/finish/pallas_call | solution.py:638

commit v6 on v5

--- a/solution.py
+++ b/solution.py
@@ -135,30 +135,42 @@
     peers += [at_x((x + d) % 4) for d in range(1, 4)]
     peers += [partner]
     source = x == y
-    load_m = pltpu.make_async_copy(m_hbm.at[0], mv, load.at[0])
-    load_g = pltpu.make_async_copy(g_hbm.at[0], gv, load.at[1])
-    load_r = pltpu.make_async_copy(r_hbm, rv, load.at[2])
+    cuts = (slice(0, 80), slice(80, SHARD))
+    loads = []
+    for i, (first, count) in enumerate(((0, 80), (80, SHARD - 80))):
+        part = pl.ds(first, count)
+        loads.append(
+            (
+                pltpu.make_async_copy(m_hbm.at[0, part], mv.at[part], load.at[2 * i]),
+                pltpu.make_async_copy(g_hbm.at[0, part], gv.at[part], load.at[2 * i + 1]),
+            )
+        )
+    load_r = pltpu.make_async_copy(r_hbm, rv, load.at[4])
 
     @pl.when(source)
     def _():
         load_r.start()
 
-    load_m.start()
-    load_g.start()
+    for load_m, load_g in loads:
+        load_m.start()
+        load_g.start()
     barrier = pltpu.get_barrier_semaphore()
     for peer in peers:
         pl.semaphore_signal(barrier, inc=1, device_id=peer, device_id_type=MESH)
 
-    load_m.wait()
-    load_g.wait()
+    for (load_m, load_g), part in zip(loads, cuts, strict=True):
+        load_m.wait()
+        load_g.wait()
+        for q in range(4):
+            columns = slice(q * BLOCK, (q + 1) * BLOCK)
+            piece = mv[part, columns] + gv[part, columns].astype(f32)
+            buffer[part, columns] = piece
+            for t in range(4):
+                bs[q, t * SHARD + part.start : t * SHARD + part.stop] = piece[:, t * 128 : (t + 1) * 128]
     for q in range(4):
-        columns = slice(q * BLOCK, (q + 1) * BLOCK)
-        part = mv[:, columns] + gv[:, columns].astype(f32)
-        buffer[:, columns] = part
-        for t in range(4):
-            bs[q, t * SHARD : (t + 1) * SHARD] = part[:, t * 128 : (t + 1) * 128]
-        bs[q, 4 * SHARD :, :64] = part[: SHARD // 2, 512:]
-        bs[q, 4 * SHARD :, 64:] = part[SHARD // 2 :, 512:]
+        columns = slice(q * BLOCK + 512, (q + 1) * BLOCK)
+        bs[q, 4 * SHARD :, :64] = buffer[: SHARD // 2, columns]
+        bs[q, 4 * SHARD :, 64:] = buffer[SHARD // 2 :, columns]
 
     @pl.when(source)
     def _():
@@ -498,7 +510,7 @@
 def exchange(momentum, gradient, right_factor):
     sem = pltpu.SemaphoreType.DMA
     longer = PACKED - PACKED // 2 // 8 * 8
-    counts = (3, 1, 3, 1, 1, 1, 3, 1, 1, 1, 3, 1, 1, 1, 2, 1, 1, 1, 2, 1, 6, 1, 16) + (1,) * 8
+    counts = (5, 1, 3, 1, 1, 1, 3, 1, 1, 1, 3, 1, 1, 1, 2, 1, 1, 1, 2, 1, 6, 1, 16) + (1,) * 8
     return pl.pallas_call(
         exchange_kernel,
         name="exchange",
@@ -558,12 +570,13 @@
 
 def finish_kernel(
     buffer, p_ref, mall, a_ref, x_first, scale, first_size, new_m, update, new_f,
-    x_ref, w_ref, top_ref, rest_ref, m_buf, u_buf, m_sem, u_sem,
+    x_ref, w_ref, own_ref, top_ref, rest_ref, m_buf, u_buf, m_sem, u_sem,
 ):
     x, z, c = (lax.axis_index(name) for name in FSDP)
 
     row, col = positions()
     x_ref[...] = x_first[...]
+    own_ref[...] = jnp.zeros_like(own_ref)
 
     def again(state):
         error = invert_step(a_ref, x_ref, FULL)
@@ -604,16 +617,17 @@
         rest_ref[q * BLOCK : (q + 1) * BLOCK] = rest
         squares = squares + jnp.sum(factor * factor, axis=0, keepdims=True)
     norms = jnp.sqrt(squares + epsilon)
-    orthonormal = dot(p_ref[...], inverse, ((1,), (1,)))
-    directions = orthonormal / norms * math.sqrt(ROWS * COLS / RANK)
-
     place = x * 32 + z * 2 + c
     for j in range(4):
 
         @pl.when(place % 4 == j)
         def _():
-            own = mall[place // 32, (place % 32) // 4, OWN * j : OWN * (j + 1)]
-            new_f[...] = dot(own, inverse, ((1,), (1,))) * (1.0 / REPLICAS) / norms
+            own_ref[:OWN] = mall[place // 32, (place % 32) // 4, OWN * j : OWN * (j + 1)]
+
+    solved = dot(jnp.concatenate([p_ref[...], own_ref[...]], axis=0), inverse, ((1,), (1,)))
+    orthonormal = solved[:SHARD]
+    new_f[...] = solved[SHARD : SHARD + OWN] * (1.0 / REPLICAS) / norms
+    directions = orthonormal / norms * math.sqrt(ROWS * COLS / RANK)
 
     both = split(jnp.concatenate([orthonormal, directions], axis=0))
     width = 256
@@ -648,6 +662,7 @@
         scratch_shapes=[
             VMEM((RANK, RANK), f32),
             VMEM((RANK, RANK), f32),
+            VMEM((24, RANK), f32),
             VMEM((COLS, RANK), jnp.bfloat16),
             VMEM((COLS, RANK), jnp.bfloat16),
             VMEM((SHARD, COLS), f32),

time: 83.1 us -> 83.3 us (level)
  no operation moved by 1% of the time
where the time goes in v6:
time: 83.3 us; the launch traced here: 82.6 us
  Pallas kernels  82 us (98%)
    pallas_call x1, Pallas kernels, exchange(): pl.pallas_call(exchange_kernel, name='exchange', out_shape=(jax.ShapeDtyp...  76.8 us
    pallas_call x1, Pallas kernels, finish(): pl.pallas_call(finish_kernel, name='finish', out_shape=(jax.ShapeDtypeStr...  5.23 us

profile of v6, /device:TPU:1, one launch (start us, length us, event | category | flops | bytes accessed | tf_op | source)
XLA Modules:
  0.0 82.6 jit_solution(8445547377809079537)
XLA Ops:
  0.6 76.8 %exchange.1 = (f32[144,2304]{1,0:T(8,128)S(1)}, f32[144,256]{1,0:T(8,128)S(1)}, f32[4,8,72,256]{3,2,1,0:T(8,128)S(1)}, f32[256,256]{1,0:T(8,128)S(1)}, f32[256,2...) custom-call(f32[1,144,2304]{2,1,0:T(8,128)} %m_hbm.1, bf16[1,144,2304]{2,1,0:T(8,128)(2,1)} %g_hbm.1, ...), custom_call_target="tpu_custom_call" | custom-call | tf_op jit(solution)/shard_map/exchange/pallas_call | solution.py:514
  77.4 5.2 %finish.1 = (f32[1,144,2304]{2,1,0:T(8,128)}, bf16[144,2304]{1,0:T(8,128)(2,1)}, f32[18,256]{1,0:T(8,128)}) custom-call(f32[144,2304]{1,0:T(8,128)S(1)} %get-tuple-element.10.buffer, f32[144,256]{1,0:T(8,128)S(1)} %get-tuple-element.11.p_ref, f32[4,8,72,256]{3,2,1,0:T(8,128)S(1)} %get-tuple-element.12.mall, f32[256,256]{1,0:T(8,128)S(1)} %get-tuple-element.13.a_ref, ...), custom_call_target="tpu_custom_call" | custom-call | tf_op jit(solution)/shard_map/finish/pallas_call | solution.py:652
